TPU v7x, 32 devices: a whole 2x2x4 slice. The times are simulated.
32 devices in a mesh: dp: 16 (over z, y, x), tensor: 2 (over core).
Axes of the slice: x: 2, y: 2, z: 4, core: 2. Of those that a mesh axis runs over, the one named last changes fastest.
Arguments:
- inputs: bfloat16 [4, 8192, 768], P(None, ('dp', 'tensor')), may hold values from -6 to 6
- lengths: int32 [4, 16], P(None, 'dp'), may hold values from 128 to 512, as said below
- bounds: int32 [4, 16], P(None, 'dp'), may hold values from 32 to 384, as said below
- query_matrix: bfloat16 [768, 768], P('dp', 'tensor'), may hold values from -0.21875 to 0.21875
- key_matrix: bfloat16 [768, 768], P('dp', 'tensor'), may hold values from -0.21875 to 0.21875
- value_matrix: bfloat16 [768, 768], P('dp', 'tensor'), may hold values from -0.21875 to 0.21875
- query_value_bias: float32 [2, 768], P(None, 'tensor'), may hold values from -3 to 3
- adapter_down_weight: bfloat16 [2, 768, 8], P(None, 'dp'), may hold values from -0.21875 to 0.21875
- adapter_up_weight: bfloat16 [2, 8, 768], P(None, None, 'tensor'), may hold values from -1 to 1
- attention_output_weight: bfloat16 [768, 768], P('tensor', 'dp'), may hold values from -1.75 to 1.75
- feedforward_input_weight: bfloat16 [768, 3072], P('dp', 'tensor'), may hold values from -0.21875 to 0.21875
- feedforward_input_bias: float32 [3072], P('tensor'), may hold values from -3 to 3
- feedforward_output_weight: bfloat16 [3072, 768], P('tensor', 'dp'), may hold values from -0.109375 to 0.109375
- output_bias: float32 [2, 768], replicated, may hold values from -3 to 3
- layernorm_scale: float32 [2, 768], replicated, may hold values from 0.5 to 1.5
- layernorm_bias: float32 [2, 768], replicated, may hold values from -2 to 2
- output_gradient: bfloat16 [4, 8192, 768], P(None, ('dp', 'tensor')), may hold values from -6 to 6
Outputs:
- outputs: bfloat16 [4, 8192, 768], P(None, ('dp', 'tensor'))
- input_grad: float32 [4, 8192, 768], P(None, ('dp', 'tensor'))
- lora_up_grad: float32 [2, 8, 768], P(None, None, 'tensor')
Inputs may be any that keep to these rules, and one draw needn't show every extreme that they name: Item i of micro-batch m has live positions 0 to lengths[m, i] - 1 of its 512; the others are padding. An item's first segment is positions 0 to bounds - 1, its second bounds to 511; bounds lies between lengths // 4 and 3 * lengths // 4.
All inputs are finite; a program needn't handle non-finite values.
Results may differ from a plain program's by a relative error of at most 0.015.
The roundings to bfloat16 on the way count: a program that leaves them out, or rounds other values in their place, can miss the bound.
Values may be sent and summed in bfloat16 or wider, within the bound.
No kernel may reach another device: no remote copies, remote signals or barrier semaphores. Data moves between devices by JAX's collectives and lax.ppermute only.
A program may use at most 192 MiB of HBM per device.

v0:
```python
import functools

import jax
import jax.numpy as jnp
from jax import lax
from jax.experimental import pallas as pl
from jax.experimental.pallas import tpu as pltpu
from jax.sharding import PartitionSpec as P

F32 = jnp.float32
BF16 = jnp.bfloat16
HEAD_DIM = 64
RANK = 8
LANES = 128
EPS = 1e-05
MASKED = -float(2**30)
SEG = 64
VMEM_LIMIT = 60 * 2**20

NT = (((1,), (1,)), ((), ()))
TN = (((0,), (0,)), ((), ()))


def mm(a, b):
    return jnp.dot(a, b, preferred_element_type=F32)


def mm_nt(a, b):
    return lax.dot_general(a, b, NT, preferred_element_type=F32)


def mm_tn(a, b):
    return lax.dot_general(a, b, TN, preferred_element_type=F32)


def iota(shape, dimension):
    return lax.broadcasted_iota(jnp.int32, shape, dimension)


def three_parts(value, lane):
    high = value.astype(BF16).astype(F32)
    rest = value - high
    middle = rest.astype(BF16).astype(F32)
    return jnp.where(lane < 16, high, jnp.where(lane < 32, middle, jnp.where(lane < 48, rest - middle, 0.0)))


def two_parts(value):
    high = value.astype(BF16)
    return jnp.concatenate([high, (value - high.astype(F32)).astype(BF16)], axis=1)


def weight_copies(order, offsets, pieces, target, sem, columns):
    firsts, blocks = order
    copies, waits = [], []
    for half, first, width, to in columns:
        for index, ref in enumerate(pieces[half]):
            rows = ref.shape[0] // blocks
            for place in range(blocks):
                start = offsets[firsts[half] + index * blocks + place]
                if rows % 16 == 0:
                    start = pl.multiple_of(start, 16)
                copies.append(
                    pltpu.make_async_copy(
                        ref.at[pl.ds(place * rows, rows), pl.ds(first, width)],
                        target.at[pl.ds(start, rows), pl.ds(to, width)],
                        sem,
                    )
                )
        filled = target.at[pl.ds(0, sum(ref.shape[0] for ref in pieces[half])), pl.ds(to, width)]
        waits.append(pltpu.make_async_copy(filled, filled, sem))
    return copies, waits


def start_all(group):
    for copy in group[0]:
        copy.start()


def wait_all(group):
    for copy in group[1]:
        copy.wait()


def places(core, shape, half_slot):
    row = iota(shape, 0)
    return jnp.where(row < half_slot, row + core * half_slot, row - core * half_slot)


def flags_of(core, length, bound, slot):
    lane = iota((slot, LANES), 1)
    place = places(core, (slot, LANES), slot // 2)
    second = place >= bound
    query = jnp.where(
        lane == SEG,
        jnp.where(second, 1.0, 0.0),
        jnp.where(lane == SEG + 1, jnp.where(second, 0.0, 1.0), jnp.where(lane == SEG + 2, 1.0, 0.0)),
    )
    key = jnp.where(
        lane == SEG,
        jnp.where(second, 0.0, MASKED),
        jnp.where(
            lane == SEG + 1,
            jnp.where(second, MASKED, 0.0),
            jnp.where((lane == SEG + 2) & (place >= length), MASKED, 0.0),
        ),
    )
    return lane, query, key


def pair_columns(pair, heads):
    per_half = heads // LANES
    base = (pair // per_half) * 3 * heads + (pair % per_half) * LANES
    return base, base + heads, base + 2 * heads


def load_projections(order, offsets, pieces, weights, sem, heads, downs):
    wide = 3 * heads
    columns = [(0, 0, wide, 0), (1, 0, wide, wide)]
    columns += [(0, wide, LANES, to) for to in downs]
    return weight_copies(order, offsets, pieces, weights, sem, columns)


def ups(up_refs, heads):
    blank = jnp.zeros((RANK, heads), BF16)
    parts = []
    for ref in up_refs:
        parts += [
            jnp.concatenate([ref[0] * 2, blank], axis=0),
            jnp.concatenate([blank, blank], axis=0),
            jnp.concatenate([blank, ref[1] * 2], axis=0),
        ]
    return jnp.concatenate(parts, axis=1)


def project_attend_kernel(order, n, offsets, lengths, bounds, core_ref, *refs):
    pieces = (refs[:n], refs[n : 2 * n])
    (
        x_own_ref,
        x_got_ref,
        bias_ref,
        up_own_ref,
        up_got_ref,
        qkv_ref,
        mixed_ref,
        spare_ref,
        low_ref,
        weights,
        down,
        sems,
    ) = refs[2 * n :]
    item = pl.program_id(0)
    core = core_ref[0]
    slot, width = mixed_ref.shape[1:]
    heads = width // 2

    @pl.when(item == 0)
    def _():
        wide = 3 * heads
        copies = weight_copies(order, offsets, pieces, weights, sems.at[0], [(0, 0, wide, 0), (1, 0, wide, wide)])
        downs = weight_copies(order, offsets, pieces, down, sems.at[1], [(0, wide, LANES, 0)])
        start_all(downs)
        start_all(copies)
        weights[width:] = jnp.zeros((2 * LANES, 6 * heads), BF16)
        up = ups((up_own_ref, up_got_ref), heads)
        weights[width : width + 2 * RANK] = up
        weights[width + LANES : width + LANES + 2 * RANK] = up
        wait_all(downs)
        wait_all(copies)

    x = jnp.concatenate([x_own_ref[0], x_got_ref[0]], axis=0)
    low = two_parts(mm(x, down[...]))
    low_ref[0] = low
    wide_x = jnp.concatenate([x, low], axis=1)
    for part in range(3):
        at = slice(part * width, (part + 1) * width)
        out = (mm(wide_x, weights[:, at]) + bias_ref[0:1, at]) * bias_ref[1:2, at]
        qkv_ref[0, :, at] = out.astype(BF16)

    lane, query_flags, key_flags = flags_of(core, lengths[item], bounds[item], slot)
    query_low = query_flags.astype(BF16)
    key_low = key_flags.astype(BF16)
    ones = jnp.where(lane == 0, 1.0, 0.0).astype(BF16)
    zero = jnp.zeros((slot, LANES), BF16)
    totals = jnp.ones((slot, LANES), F32)
    peaks = []
    for pair in range(width // LANES):
        at_query, at_key, at_value = pair_columns(pair, heads)
        query = qkv_ref[0, :, at_query : at_query + LANES]
        keys = jnp.concatenate([qkv_ref[0, :, at_key : at_key + LANES], key_low], axis=1)
        values = jnp.concatenate([qkv_ref[0, :, at_value : at_value + LANES], ones], axis=1)
        outs = []
        for side in range(2):
            inside = (lane < HEAD_DIM) if side == 0 else (lane >= HEAD_DIM)
            query_side = jnp.concatenate([jnp.where(inside, query, zero), query_low], axis=1)
            scores = mm_nt(keys, query_side)
            peak = jnp.max(scores, axis=0, keepdims=True)
            probs = jnp.exp(scores - peak).astype(BF16)
            out = mm_tn(probs, values)
            total = out[:, LANES : LANES + 1]
            outs.append(out[:, :LANES] * (1.0 / total))
            totals = jnp.where((lane & 15) == 2 * pair + side, total, totals)
            peaks.append(peak)
        mixed_ref[0, :, pair * LANES : (pair + 1) * LANES] = jnp.where(
            lane < HEAD_DIM, outs[0], outs[1]
        ).astype(BF16)
    peaks += [jnp.zeros((1, slot), F32)] * (16 - len(peaks))
    peaks = jnp.concatenate(peaks, axis=0)
    peaks = jnp.concatenate([peaks] * (LANES // 16), axis=0).T
    spare_ref[0] = (three_parts(peaks + jnp.log(totals), lane) + query_flags).astype(BF16)


def row_mean(value):
    return jnp.mean(value, axis=-1, keepdims=True)


def normalize(value):
    centre = value - row_mean(value)
    scale = lax.rsqrt(row_mean(centre * centre) + EPS)
    return centre * scale, scale


def normalize_back(grad, gain, normal, scale):
    grad = grad * gain
    return scale * (grad - row_mean(grad) - normal * row_mean(grad * normal))


def feed_kernel(orders, chunks, n, offsets, core_ref, *refs):
    pieces = (refs[:n], refs[n : 2 * n])
    pieces_last = (refs[2 * n : 3 * n], refs[3 * n : 4 * n])
    (
        x_own_ref,
        x_got_ref,
        mixed_ref,
        grad_own_ref,
        grad_got_ref,
        hidden_bias_ref,
        output_bias_ref,
        gain_ref,
        shift_ref,
        out_own_ref,
        out_got_ref,
        grad_hidden_ref,
        grad_mixed_ref,
        out_weights,
        in_weights,
        back_weights,
        slope,
        sems,
    ) = refs[4 * n :]
    slot, width = mixed_ref.shape[1:]
    half_slot = slot // 2
    heads = width // 2
    first, last = chunks
    size = width
    parts = list(range(0, 2 * (first + last), size))

    o = heads
    tail = 2 * first
    groups = [
        weight_copies(orders[0], offsets, pieces, out_weights, sems.at[0], [(0, 0, o, 0), (1, 0, o, o)]),
        weight_copies(orders[0], offsets, pieces, in_weights, sems.at[1], [(0, o, first, 0), (1, o, first, first)]),
        weight_copies(
            orders[0], offsets, pieces, back_weights, sems.at[2], [(0, o + first, first, 0), (1, o + first, first, first)]
        ),
        weight_copies(
            orders[1], offsets, pieces_last, in_weights, sems.at[3], [(0, 0, last, tail), (1, 0, last, tail + last)]
        ),
        weight_copies(
            orders[1], offsets, pieces_last, back_weights, sems.at[4], [(0, last, last, tail), (1, last, last, tail + last)]
        ),
    ]

    @pl.when(pl.program_id(0) == 0)
    def _():
        for group in groups:
            start_all(group)

    def arrived(*which):
        @pl.when(pl.program_id(0) == 0)
        def _():
            for index in which:
                wait_all(groups[index])

    arrived(0)
    x = jnp.concatenate([x_own_ref[0], x_got_ref[0]], axis=0).astype(F32)
    summed = x + output_bias_ref[0:1] + mm_nt(mixed_ref[0], out_weights[...])
    normal_in, scale_in = normalize(summed)
    normed = normal_in * gain_ref[0:1] + shift_ref[0:1]
    normed_low = normed.astype(BF16)
    total = normed + output_bias_ref[1:2]
    for at in parts:
        if at == 0:
            arrived(1)
        if at < tail < at + size or at == tail:
            arrived(3)
        pre = mm(normed_low, in_weights[:, at : at + size]) + hidden_bias_ref[:, at : at + size]
        share = 0.5 * (1.0 + lax.erf(pre * 0.7071067811865476))
        slope[:, at : at + size] = share + pre * jnp.exp(-0.5 * pre * pre) * 0.3989422804014327
        if at == 0:
            arrived(2)
        if at < tail < at + size or at == tail:
            arrived(4)
        total += mm_nt((pre * share).astype(BF16), back_weights[:, at : at + size])
    normal_out, scale_out = normalize(total)
    out = (normal_out * gain_ref[1:2] + shift_ref[1:2]).astype(BF16)
    out_own_ref[0] = out[:half_slot]
    out_got_ref[0] = out[half_slot:]
    grad = jnp.concatenate([grad_own_ref[0], grad_got_ref[0]], axis=0).astype(F32)
    grad_total = normalize_back(grad, gain_ref[1:2], normal_out, scale_out)
    grad_low = grad_total.astype(BF16)
    grad_normed = grad_total
    for at in parts:
        grad_pre = (mm(grad_low, back_weights[:, at : at + size]) * slope[:, at : at + size]).astype(BF16)
        grad_normed += mm_nt(grad_pre, in_weights[:, at : at + size])
    grad_hidden = normalize_back(grad_normed, gain_ref[0:1], normal_in, scale_in)
    grad_hidden_ref[0] = grad_hidden
    grad_mixed_ref[0] = mm(grad_hidden.astype(BF16), out_weights[...]).astype(BF16)


def attend_back_kernel(lengths, bounds, core_ref, *refs):
    (
        qkv_ref,
        mixed_ref,
        spare_ref,
        low_ref,
        grad_mixed_ref,
        grads_ref,
        adapter_ref,
    ) = refs
    item = pl.program_id(0)
    core = core_ref[0]
    slot, width = mixed_ref.shape[1:]
    heads = width // 2

    lane, _, key_flags = flags_of(core, lengths[item], bounds[item], slot)
    row = iota((width, LANES), 0)
    column = iota((width, LANES), 1)
    pick = jnp.where((row // HEAD_DIM == (column & 15)) & (column < 48), 1.0, 0.0).astype(BF16)
    product = grad_mixed_ref[0].astype(F32) * mixed_ref[0].astype(F32)
    high = product.astype(BF16)
    rest = (product - high.astype(F32)).astype(BF16)
    inner = three_parts(mm(high, pick) + mm(rest, pick), lane).astype(BF16)
    spare = spare_ref[0]
    zero = jnp.zeros((slot, LANES), BF16)
    per_half = heads // LANES

    def columns(first):
        return pl.ds(pl.multiple_of(first, LANES), LANES)

    def of_pair(pair):
        base = (pair // per_half) * 3 * heads + (pair % per_half) * LANES
        at_query, at_key, at_value = (columns(base + part * heads) for part in range(3))
        query = qkv_ref[0, :, at_query]
        keys = qkv_ref[0, :, at_key]
        values = qkv_ref[0, :, at_value]
        grad = grad_mixed_ref[0, :, columns(pair * LANES)]
        total_query = jnp.zeros((slot, LANES), F32)
        total_key = jnp.zeros((slot, LANES), F32)
        total_value = jnp.zeros((slot, LANES), F32)
        for side in range(2):
            head = 2 * pair + side
            inside = (lane < HEAD_DIM) if side == 0 else (lane >= HEAD_DIM)
            mine = ((lane & 15) == head) & (lane < 48)
            query_side = jnp.where(inside, query, zero)
            key_side = jnp.where(inside, keys, zero)
            grad_side = jnp.where(inside, grad, zero)
            key_wide = jnp.concatenate([keys, jnp.where(mine, -1.0, key_flags).astype(BF16)], axis=1)
            value_wide = jnp.concatenate([values, jnp.where(mine, -1.0, 0.0).astype(BF16)], axis=1)
            probs = jnp.exp(mm_nt(key_wide, jnp.concatenate([query_side, spare], axis=1)))
            grad_probs = mm_nt(value_wide, jnp.concatenate([grad_side, inner], axis=1))
            grad_scores = (probs * grad_probs).astype(BF16)
            total_value += mm(probs.astype(BF16), grad_side)
            total_key += mm(grad_scores, query_side)
            total_query += mm_tn(grad_scores, key_side)
        grads_ref[0, :, at_query] = (total_query * 0.125).astype(BF16)
        grads_ref[0, :, at_key] = total_key.astype(BF16)
        grads_ref[0, :, at_value] = total_value.astype(BF16)

    pairs = width // LANES
    group = 3 if pairs % 3 == 0 else 1

    @pl.loop(0, pairs // group)
    def _(step):
        for place in range(group):
            of_pair(step * group + place)

    update = 2.0 * mm_tn(low_ref[0], grads_ref[0])
    parts = []
    for half in range(2):
        at = half * 3 * heads
        of_query = update[:, at : at + heads]
        of_value = update[:, at + 2 * heads : at + 3 * heads]
        rows = [
            of_query[:RANK] + of_query[LANES : LANES + RANK],
            of_value[RANK : 2 * RANK] + of_value[LANES + RANK : LANES + 2 * RANK],
        ]
        parts.append(jnp.concatenate(rows, axis=0))
    part = jnp.concatenate(parts, axis=1)

    @pl.when(item == 0)
    def _():
        adapter_ref[...] = part

    @pl.when(item > 0)
    def _():
        adapter_ref[...] += part


def input_grad_kernel(order, n, offsets, core_ref, *refs):
    pieces = (refs[:n], refs[n : 2 * n])
    (
        grads_ref,
        grad_hidden_ref,
        up_own_ref,
        up_got_ref,
        own_ref,
        got_ref,
        weights,
        up,
        sems,
    ) = refs[2 * n :]
    slot, width = grad_hidden_ref.shape[1:]
    heads = width // 2

    @pl.when(pl.program_id(0) == 0)
    def _():
        copies = load_projections(order, offsets, pieces, weights, sems.at[0], heads, (6 * heads, 6 * heads + LANES))
        start_all(copies)
        up[...] = jnp.zeros_like(up)
        up[: 2 * RANK] = ups((up_own_ref, up_got_ref), heads)
        wait_all(copies)

    grads = grads_ref[0]
    small = two_parts(mm_nt(grads, up[...]))
    total = grad_hidden_ref[0] + mm_nt(jnp.concatenate([grads, small], axis=1), weights[...])
    own_ref[0] = total[: slot // 2]
    got_ref[0] = total[slot // 2 :]


def any_spec():
    return pl.BlockSpec(memory_space=pl.ANY)


def whole_spec(array):
    return pl.BlockSpec(array.shape, lambda i, *_: (0,) * array.ndim)


def item_spec(shape):
    return pl.BlockSpec((1, *shape[1:]), lambda i, *_: (i, 0, 0))


def shape_of(shape, dtype):
    return jax.ShapeDtypeStruct(shape, dtype)


def call(kernel, name, scalars, flat, args, outs, scratch, items, flops, moved):
    return pl.pallas_call(
        kernel,
        grid_spec=pltpu.PrefetchScalarGridSpec(
            num_scalar_prefetch=len(scalars),
            grid=(items,),
            in_specs=[any_spec()] * len(flat) + [spec for _, spec in args],
            out_specs=[spec for _, spec in outs],
            scratch_shapes=scratch,
        ),
        out_shape=[shape for shape, _ in outs],
        compiler_params=pltpu.CompilerParams(vmem_limit_bytes=VMEM_LIMIT),
        cost_estimate=pl.CostEstimate(flops=flops, bytes_accessed=moved, transcendentals=0),
        name=name,
    )(*scalars, *flat, *[array for array, _ in args])


def swap(array):
    return lax.ppermute(array, "tensor", [(0, 1), (1, 0)])


def after(value, *deps):
    return lax.optimization_barrier((value, *deps))[0]


def over_dp(count, array, target):
    return lax.ppermute(array, "dp", [(i, target(i)) for i in range(count)])


LINE_FIRST = ((4, 8, 1, 2), (8, 4, 2, 1))
PLANE_FIRST = ((1, 2, 4, 8), (2, 1, 8, 4))


def block_offsets(index, rows, flips):
    place = jnp.arange(16)
    flipped = sum(((place >> bit) & 1) * flips[bit] for bit in range(4))
    return ((index ^ flipped) * rows).astype(jnp.int32)


def local(
    inputs,
    lengths,
    bounds,
    query_matrix,
    key_matrix,
    value_matrix,
    query_value_bias,
    adapter_down_weight,
    adapter_up_weight,
    attention_output_weight,
    feedforward_input_weight,
    feedforward_input_bias,
    feedforward_output_weight,
    output_bias,
    layernorm_scale,
    layernorm_bias,
    output_gradient,
    *,
    count,
):
    micro, rows, width = inputs.shape
    mine = micro // 2
    slot = 2 * rows
    heads = width // 2
    core = lax.axis_index("tensor")
    shard_rows = query_matrix.shape[0]
    hidden = feedforward_input_weight.shape[1]
    last = hidden // 3 if count == 16 else hidden // 2
    first = hidden - last

    down = jnp.transpose(adapter_down_weight, (1, 0, 2)).reshape(shard_rows, 2 * RANK)
    down = jnp.pad(down, ((0, 0), (0, LANES - 2 * RANK)))
    shard = jnp.concatenate([query_matrix, key_matrix, value_matrix, down], axis=1)
    back = feedforward_output_weight.T
    shard_first = jnp.concatenate(
        [attention_output_weight.T, feedforward_input_weight[:, :first], back[:, :first]], axis=1
    )
    shard_last = jnp.concatenate([feedforward_input_weight[:, first:], back[:, first:]], axis=1)

    others = (1 - core) * mine
    x_got = swap(lax.dynamic_slice_in_dim(inputs, others, mine, 0))
    grad_got = swap(lax.dynamic_slice_in_dim(output_gradient, others, mine, 0))
    bias_got, up_got, hidden_bias_got = map(swap, (query_value_bias, adapter_up_weight, feedforward_input_bias))

    blank = jnp.zeros((heads,), F32)
    ones = blank + 1
    both = [query_value_bias[0], blank, query_value_bias[1], bias_got[0], blank, bias_got[1]]
    scale = [ones * 0.125, ones, ones] * 2
    bias = jnp.stack([jnp.concatenate(both), jnp.concatenate(scale)])

    if count == 16:
        index = lax.axis_index("dp")

        def tables(flips):
            mine_first = [jnp.where(core == 0, a, b) for a, b in zip(*flips, strict=True)]
            other_first = [jnp.where(core == 0, b, a) for a, b in zip(*flips, strict=True)]
            return [block_offsets(index, shard_rows, f) for f in (mine_first, other_first)]

        offsets = jnp.concatenate(tables(LINE_FIRST) + tables(PLANE_FIRST))
        order, order_last, n = ((0, 16), 8), ((32, 48), 8), 2

        def exchange(array, flips, step):
            pairs = [(2 * i + t, 2 * (i ^ flips[t][step]) + t) for i in range(count) for t in range(2)]
            return lax.ppermute(array, ("dp", "tensor"), pairs)

        def joined(*arrays):
            return jnp.concatenate(arrays, axis=0)

        line = joined(shard, exchange(shard, LINE_FIRST, 0))
        line, shard_last = lax.optimization_barrier((line, shard_last))
        plane = joined(shard_last, exchange(shard_last, PLANE_FIRST, 0))
        line = joined(line, exchange(line, LINE_FIRST, 1))
        line, plane, *early = lax.optimization_barrier((line, plane, x_got, up_got, grad_got, hidden_bias_got, offsets, bias))
        x_got, up_got, grad_got, hidden_bias_got, offsets, bias = early
        shard_first = after(shard_first, line)
        line_first = joined(shard_first, exchange(shard_first, LINE_FIRST, 0))
        plane = joined(plane, exchange(plane, PLANE_FIRST, 1))
        line = joined(line, exchange(line, LINE_FIRST, 2))
        line, plane, line_first = lax.optimization_barrier((line, plane, line_first))
        line_first = joined(line_first, exchange(line_first, LINE_FIRST, 1))
        own = [line, exchange(line, LINE_FIRST, 3)]
        swapped = [swap(line)]
        line_first, plane, own, swapped = lax.optimization_barrier((line_first, plane, own, swapped))
        swapped.append(swap(own[1]))
        line_first = joined(line_first, exchange(line_first, LINE_FIRST, 2))
        plane = joined(plane, exchange(plane, PLANE_FIRST, 2))
        plane, line_first, x_got, swapped = lax.optimization_barrier((plane, line_first, x_got, swapped))
        own_first = [line_first, exchange(line_first, LINE_FIRST, 3)]
        own_last = [plane, exchange(plane, PLANE_FIRST, 3)]
        got_first, got_last = [swap(line_first)], [swap(plane)]
    else:
        offsets = jnp.zeros((2,), jnp.int32)
        order = order_last = ((0, 0), 1)
        n = 1
        own, own_first, own_last = (
            [lax.all_gather(s, "dp", axis=0, tiled=True)] for s in (shard, shard_first, shard_last)
        )
        swapped, got_first, got_last = [swap(own[0])], [], []
    pieces = (*own, *swapped)

    first_item = core * mine
    my_lengths = lax.dynamic_slice_in_dim(lengths[:, 0], first_item, mine, 0)
    my_bounds = lax.dynamic_slice_in_dim(bounds[:, 0], first_item, mine, 0)
    core = core[None].astype(jnp.int32)

    own_block = pl.BlockSpec((1, rows, width), lambda i, *s: (s[-1][0] * mine + i, 0, 0))
    got_block = pl.BlockSpec((1, rows, width), lambda i, *_: (i, 0, 0))
    item = (mine, slot, width)
    wide = (mine, slot, 3 * width)

    def out_item(shape, dtype):
        return shape_of(shape, dtype), item_spec(shape)

    def in_item(array):
        return array, item_spec(array.shape)

    def in_whole(array):
        return array, whole_spec(array)

    split_out = lambda dtype: [(shape_of(inputs.shape, dtype), own_block), (shape_of((mine, rows, width), dtype), got_block)]

    tokens = mine * slot
    qkv, mixed, spare, low = call(
        functools.partial(project_attend_kernel, order, n),
        "project_attend",
        (offsets, my_lengths, my_bounds, core),
        pieces,
        [(inputs, own_block), (x_got, got_block), in_whole(bias), in_whole(adapter_up_weight), in_whole(up_got)],
        [
            out_item(wide, BF16),
            out_item(item, BF16),
            out_item((mine, slot, LANES), BF16),
            out_item((mine, slot, 2 * LANES), BF16),
        ],
        [
            pltpu.VMEM((width + 2 * LANES, 3 * width), BF16),
            pltpu.VMEM((width, LANES), BF16),
            pltpu.SemaphoreType.DMA((2,)),
        ],
        mine,
        2 * tokens * width * (4 * width + 8 * slot),
        12 * tokens * width,
    )
    own_first, own_last = lax.optimization_barrier((own_first, own_last, mixed))[:2]
    got_first += map(swap, own_first[len(got_first) :])
    got_last += map(swap, own_last[len(got_last) :])
    hidden_bias = jnp.concatenate(
        [
            feedforward_input_bias[:first],
            hidden_bias_got[:first],
            feedforward_input_bias[first:],
            hidden_bias_got[first:],
        ]
    )[None]
    pieces_feed = (*own_first, *got_first, *own_last, *got_last)
    out, out_send, grad_hidden, grad_mixed = call(
        functools.partial(feed_kernel, (order, order_last), (first, last), n),
        "feed",
        (offsets, core),
        pieces_feed,
        [
            (inputs, own_block),
            (x_got, got_block),
            in_item(mixed),
            (output_gradient, own_block),
            (grad_got, got_block),
            *map(in_whole, (hidden_bias, output_bias, layernorm_scale, layernorm_bias)),
        ],
        [*split_out(BF16), out_item(item, F32), out_item(item, BF16)],
        [
            pltpu.VMEM((width, width), BF16),
            pltpu.VMEM((width, 2 * hidden), BF16),
            pltpu.VMEM((width, 2 * hidden), BF16),
            pltpu.VMEM((slot, 2 * hidden), F32),
            pltpu.SemaphoreType.DMA((5,)),
        ],
        mine,
        4 * tokens * width * (width + 4 * hidden),
        8 * width * hidden,
    )
    out_send = swap(out_send)
    adapter = (2 * RANK, width)
    grads, adapter = call(
        attend_back_kernel,
        "attend_back",
        (my_lengths, my_bounds, core),
        (),
        [*map(in_item, (qkv, mixed, spare, low, grad_mixed))],
        [out_item(wide, BF16), (shape_of(adapter, F32), pl.BlockSpec(adapter, lambda i, *_: (0, 0)))],
        [],
        mine,
        2 * tokens * width * 20 * slot,
        16 * tokens * width,
    )
    if count == 16:
        ways = [over_dp(count, adapter, lambda i, flip=flip: i ^ flip) for flip in (4, 8, 12)]
    total, total_send = call(
        functools.partial(input_grad_kernel, order, n),
        "input_grad",
        (offsets, core),
        pieces,
        [in_item(grads), in_item(grad_hidden), in_whole(adapter_up_weight), in_whole(up_got)],
        split_out(F32),
        [
            pltpu.VMEM((width, 3 * width + 2 * LANES), BF16),
            pltpu.VMEM((LANES, 3 * width), BF16),
            pltpu.SemaphoreType.DMA((1,)),
        ],
        mine,
        2 * tokens * width * 3 * width,
        12 * tokens * width,
    )
    if count == 16:
        *ways, total_send, out = lax.optimization_barrier((*ways, total_send, out))
        adapter = (adapter + ways[0]) + (ways[1] + ways[2])
        ways = [over_dp(count, adapter, lambda i, flip=flip: i ^ flip) for flip in (1, 2, 3)]
        input_grad = lax.dynamic_update_slice_in_dim(total, swap(total_send), others, 0)
        result = lax.dynamic_update_slice_in_dim(out, out_send, others, 0)
        *ways, input_grad, result = lax.optimization_barrier((*ways, input_grad, result))
        adapter = (adapter + ways[0]) + (ways[1] + ways[2])
    else:
        adapter = lax.psum(adapter, "dp")
        input_grad = lax.dynamic_update_slice_in_dim(total, swap(total_send), others, 0)
        result = lax.dynamic_update_slice_in_dim(out, out_send, others, 0)
    adapter = adapter[:, :heads] + swap(adapter[:, heads:])
    return result, input_grad, adapter.reshape(2, RANK, heads)


def solution(mesh):
    return jax.shard_map(
        functools.partial(local, count=mesh.shape["dp"]),
        mesh=mesh,
        in_specs=(
            P(None, ("dp", "tensor"), None),
            P(None, "dp"),
            P(None, "dp"),
            P("dp", "tensor"),
            P("dp", "tensor"),
            P("dp", "tensor"),
            P(None, "tensor"),
            P(None, "dp", None),
            P(None, None, "tensor"),
            P("tensor", "dp"),
            P("dp", "tensor"),
            P("tensor"),
            P("tensor", "dp"),
            P(),
            P(),
            P(),
            P(None, ("dp", "tensor"), None),
        ),
        out_specs=(
            P(None, ("dp", "tensor"), None),
            P(None, ("dp", "tensor"), None),
            P(None, None, "tensor"),
        ),
        check_vma=False,
    )
```

profile of v0, /device:TPU:0, one launch (start us, length us, event | category | flops | bytes accessed | tf_op | source)
XLA Modules:
  0.0 186.0 jit_solution(9596183536287093065)
XLA Ops:
  2.1 1.5 pad_maximum_fusion.10
  3.6 3.0 %collective-permute-start = (bf16[48,1280]{1,0:T(8,128)(2,1)}, bf16[48,1280]{1,0:T(8,128)(2,1)}, u32[]{:S(2)}, u32[]{:S(2)}) collective-permute-start(bf16[48,1280]{1,0:T(8,128)(2,1)} %pad_maximum_fusion.10), channel_id=1, source_target_pairs={{0,8},{1,17},{2,10},{3,19},{4,12},{5,21},{6,14},{7,23},{8,0},{9,25... | collective-permute-start | bytes 368648 | tf_op jit(solution)/shard_map/ppermute | solution.py:559
  11.9 2.1 %collective-permute-start.2 = (bf16[48,1024]{1,0:T(8,128)(2,1)S(1)}, bf16[48,1024]{1,0:T(8,128)(2,1)S(1)}, u32[]{:S(2)}, u32[]{:S(2)}) collective-permute-start(bf16[48,1024]{1,0:T(8,128)(2,1)S(1)} %pad_maximum_fusion.11), channel_id=1, source_target_pairs={{0,2},{1,5},{2,0},{3,7},{4,6},{5,1},{6,4},{7,3},{8,10},{9,13},{10,... | collective-permute-start | bytes 294920 | tf_op jit(solution)/shard_map/ppermute | solution.py:559
  14.0 1.6 collective-permute-start.1
  15.6 1.3 pad_maximum_fusion.12.refs_6_
  17.0 6.8 %collective-permute-done.1 = bf16[96,1280]{1,0:T(8,128)(2,1)S(1)} collective-permute-done((bf16[96,1280]{1,0:T(8,128)(2,1)S(1)}, bf16[96,1280]{1,0:T(8,128)(2,1)S(1)}, u32[]{:S(2)}, u32[]{:S(2)}) %collective-permute-start.1) | collective-permute-done | bytes 245792 | tf_op jit(solution)/shard_map/ppermute | solution.py:559
  23.9 1.5 collective-permute-start.9
  27.1 3.9 %collective-permute-done.9 = bf16[96,1024]{1,0:T(8,128)(2,1)S(1)} collective-permute-done((bf16[96,1024]{1,0:T(8,128)(2,1)S(1)}, bf16[96,1024]{1,0:T(8,128)(2,1)S(1)}, u32[]{:S(2)}, u32[]{:S(2)}) %collective-permute-start.9) | collective-permute-done | bytes 196640 | tf_op jit(solution)/shard_map/ppermute | solution.py:559
  31.0 3.4 %collective-permute-done.10 = bf16[48,2432]{1,0:T(8,128)(2,1)S(1)} collective-permute-done((bf16[48,2432]{1,0:T(8,128)(2,1)S(1)}, bf16[48,2432]{1,0:T(8,128)(2,1)S(1)}, u32[]{:S(2)}, u32[]{:S(2)}) %collective-permute-start.10) | collective-permute-done | bytes 233504 | tf_op jit(solution)/shard_map/ppermute | solution.py:559
  36.2 3.3 %collective-permute-start.11 = (bf16[96,2432]{1,0:T(8,128)(2,1)S(1)}, bf16[96,2432]{1,0:T(8,128)(2,1)S(1)}, u32[]{:S(2)}, u32[]{:S(2)}) collective-permute-start(bf16[96,2432]{1,0:T(8,128)(2,1)S(1)} %pad_maximum_fusion.5), channel_id=1, source_target_pairs={{0,16},{1,9},{2,18},{3,11},{4,20},{5,13},{6,22},{7,15},{8,24},{9,1... | collective-permute-start | bytes 1400840 | tf_op jit(solution)/shard_map/ppermute | solution.py:559
  39.5 10.8 %collective-permute-done.11 = bf16[96,2432]{1,0:T(8,128)(2,1)S(1)} collective-permute-done((bf16[96,2432]{1,0:T(8,128)(2,1)S(1)}, bf16[96,2432]{1,0:T(8,128)(2,1)S(1)}, u32[]{:S(2)}, u32[]{:S(2)}) %collective-permute-start.11) | collective-permute-done | bytes 466976 | tf_op jit(solution)/shard_map/ppermute | solution.py:559
  50.4 1.8 collective-permute-start.15
  52.6 10.5 %collective-permute-done.14 = bf16[192,1024]{1,0:T(8,128)(2,1)S(1)} collective-permute-done((bf16[192,1024]{1,0:T(8,128)(2,1)S(1)}, bf16[192,1024]{1,0:T(8,128)(2,1)S(1)}, u32[]{:S(2)}, u32[]{:S(2)}) %collective-permute-start.14) | collective-permute-done | bytes 393248 | tf_op jit(solution)/shard_map/ppermute | solution.py:559
  66.5 2.5 %collective-permute-start.18 = (bf16[384,1024]{1,0:T(8,128)(2,1)S(1)}, bf16[384,1024]{1,0:T(8,128)(2,1)S(1)}, u32[]{:S(2)}, u32[]{:S(2)}) collective-permute-start(bf16[384,1024]{1,0:T(8,128)(2,1)S(1)} %pad_maximum_fusion.3.refs_4_), channel_id=1, source_target_pairs={{0,16},{1,9},{2,18},{3,11},{4,20},{5,13},{6,22},{7,15},{8,24},{9,1... | collective-permute-start | bytes 2359304 | tf_op jit(solution)/shard_map/ppermute | solution.py:559
  69.0 21.9 %project_attend.1 = (bf16[2,512,2304]{2,1,0:T(8,128)(2,1)}, bf16[2,512,768]{2,1,0:T(8,128)(2,1)}, bf16[2,512,128]{2,1,0:T(8,128)(2,1)}, bf16[2,512,256]{2,1,0:T(8,128)(2,1)}) custom-call(s32[64]{0:T(128)} %pad_add_fusion.offsets, s32[2]{0:T(128)} %get-tuple-element.111.lengths, s32[2]{0:T(128)} %get-tuple-element.112.bounds, s32[1]{0:T(128)} %bitcast.2.core_ref, ...), custom_call_target="tpu_custom_call" | custom-call | flops 11274289152 | bytes 9437184 | tf_op jit(solution)/shard_map/project_attend/pallas_call | solution.py:457
  93.5 2.6 %collective-permute-done.21.refs_6_ = bf16[384,1024]{1,0:T(8,128)(2,1)S(1)} collective-permute-done((bf16[384,1024]{1,0:T(8,128)(2,1)S(1)}, bf16[384,1024]{1,0:T(8,128)(2,1)S(1)}, u32[]{:S(2)}, u32[]{:S(2)}) %collective-permute-start.21) | collective-permute-done | bytes 786464 | tf_op jit(solution)/shard_map/ppermute | solution.py:474
  98.2 36.4 %feed.1 = (bf16[4,256,768]{2,1,0:T(8,128)(2,1)}, bf16[2,256,768]{2,1,0:T(8,128)(2,1)}, f32[2,512,768]{2,1,0:T(8,128)}, bf16[2,512,768]{2,1,0:T(8,128)(2,1)}) custom-call(s32[64]{0:T(128)} %pad_add_fusion.offsets, s32[1]{0:T(128)} %bitcast.2.core_ref, bf16[384,2432]{1,0:T(8,128)(2,1)} %copy-done, bf16[384,2432]{1,0:T(8,128)(2,1)} %collective-permute-done.17.refs_1_, ...), custom_call_target="tpu_custom_call" | custom-call | flops 21743271936 | bytes 9437184 | tf_op jit(solution)/shard_map/feed/pallas_call | solution.py:457
  134.6 26.1 %attend_back.1 = (bf16[2,512,2304]{2,1,0:T(8,128)(2,1)}, f32[16,768]{1,0:T(8,128)}) custom-call(s32[2]{0:T(128)} %get-tuple-element.111.lengths, s32[2]{0:T(128)} %get-tuple-element.112.bounds, s32[1]{0:T(128)} %bitcast.2.core_ref, bf16[2,512,2304]{2,1,0:T(8,128)(2,1)} %get-tuple-element.73.refs_0_, bf16[2,512,768]{2,1,0:T(8,128)(2,1)} %get-tuple-element.74.refs_10_.refs_1_, ...), custom_call_target="tpu_custom_call" | custom-call | flops 16106127360 | bytes 12582912 | tf_op jit(solution)/shard_map/attend_back/pallas_call | solution.py:457
  160.7 1.7 collective-permute-start.25
  162.4 1.4 collective-permute-start.24
  165.1 12.1 %input_grad.1 = (f32[4,256,768]{2,1,0:T(8,128)}, f32[2,256,768]{2,1,0:T(8,128)}) custom-call(s32[64]{0:T(128)} %pad_add_fusion.offsets, s32[1]{0:T(128)} %bitcast.2.core_ref, bf16[384,1280]{1,0:T(8,128)(2,1)} %copy-done.1, bf16[384,1280]{1,0:T(8,128)(2,1)} %copy-done.17, bf16[384,1280]{1,0:T(8,128)(2,1)} %copy-done.16, bf16[384,1280]{1,0:T(8,128)(2,1)} %copy-done.18, ...), custom_call_target="tpu_custom_call" | custom-call | flops 3623878656 | bytes 9437184 | tf_op jit(solution)/shard_map/input_grad/pallas_call | solution.py:457
  177.8 1.6 collective-permute-start.28
  180.0 1.3 collective-permute-start.26
  182.1 1.3 constant_dynamic-update-slice_fusion.7
  (142 shorter events, 24.3 us)
Async XLA Ops:
  0.7 9.0 %collective-permute-start.7 = (f32[2,384]{1,0:T(2,128)}, f32[2,384]{1,0:T(2,128)}, u32[]{:S(2)}, u32[]{:S(2)}) collective-permute-start(f32[2,384]{1,0:T(2,128)} %param.23), channel_id=1, source_target_pairs={{0,1},{1,0},{2,3},{3,2},{4,5},{5,4},{6,7},{7,6},{8,9},{9,8},{10,11... | collective-permute-start | bytes 9224 | tf_op jit(solution)/shard_map/ppermute | solution.py:474
  1.2 22.6 %collective-permute-start.6 = (f32[1536]{0:T(1024)}, f32[1536]{0:T(1024)}, u32[]{:S(2)}, u32[]{:S(2)}) collective-permute-start(f32[1536]{0:T(1024)} %param.28), channel_id=1, source_target_pairs={{0,1},{1,0},{2,3},{3,2},{4,5},{5,4},{6,7},{7,6},{8,9},{9,8},{10,11... | collective-permute-start | bytes 18440 | tf_op jit(solution)/shard_map/ppermute | solution.py:474
  3.6 7.3 %collective-permute-start = (bf16[48,1280]{1,0:T(8,128)(2,1)}, bf16[48,1280]{1,0:T(8,128)(2,1)}, u32[]{:S(2)}, u32[]{:S(2)}) collective-permute-start(bf16[48,1280]{1,0:T(8,128)(2,1)} %pad_maximum_fusion.10), channel_id=1, source_target_pairs={{0,8},{1,17},{2,10},{3,19},{4,12},{5,21},{6,14},{7,23},{8,0},{9,25... | collective-permute-start | bytes 368648 | tf_op jit(solution)/shard_map/ppermute | solution.py:559
  7.9 16.0 %collective-permute-start.3 = (bf16[2,256,768]{2,1,0:T(8,128)(2,1)S(1)}, bf16[2,256,768]{2,1,0:T(8,128)(2,1)}, u32[]{:S(2)}, u32[]{:S(2)}) collective-permute-start(bf16[2,256,768]{2,1,0:T(8,128)(2,1)S(1)} %constant_dynamic-slice_fusion.1), channel_id=1, source_target_pairs={{0,1},{1,0},{2,3},{3,2},{4,5},{5,4},{6,7},{7,6},{8,9},{9,8},{10,11... | collective-permute-start | bytes 2359304 | tf_op jit(solution)/shard_map/ppermute | solution.py:474
  8.7 15.1 %collective-permute-start.5 = (bf16[2,256,768]{2,1,0:T(8,128)(2,1)S(1)}, bf16[2,256,768]{2,1,0:T(8,128)(2,1)S(1)}, u32[]{:S(2)}, u32[]{:S(2)}) collective-permute-start(bf16[2,256,768]{2,1,0:T(8,128)(2,1)S(1)} %constant_dynamic-slice_fusion), channel_id=1, source_target_pairs={{0,1},{1,0},{2,3},{3,2},{4,5},{5,4},{6,7},{7,6},{8,9},{9,8},{10,11... | collective-permute-start | bytes 2359304 | tf_op jit(solution)/shard_map/ppermute | solution.py:474
  14.0 9.8 %collective-permute-start.1 = (bf16[96,1280]{1,0:T(8,128)(2,1)S(1)}, bf16[96,1280]{1,0:T(8,128)(2,1)S(1)}, u32[]{:S(2)}, u32[]{:S(2)}) collective-permute-start(bf16[96,1280]{1,0:T(8,128)(2,1)S(1)} %pad_maximum_fusion.7), channel_id=1, source_target_pairs={{0,16},{1,9},{2,18},{3,11},{4,20},{5,13},{6,22},{7,15},{8,24},{9,1... | collective-permute-start | bytes 737288 | tf_op jit(solution)/shard_map/ppermute | solution.py:559
  17.0 6.9 %collective-permute-start.4 = (bf16[2,8,384]{2,1,0:T(8,128)(2,1)}, bf16[2,8,384]{2,1,0:T(8,128)(2,1)S(1)}, u32[]{:S(2)}, u32[]{:S(2)}) collective-permute-start(bf16[2,8,384]{2,1,0:T(8,128)(2,1)} %refs_6_.1), channel_id=1, source_target_pairs={{0,1},{1,0},{2,3},{3,2},{4,5},{5,4},{6,7},{7,6},{8,9},{9,8},{10,11... | collective-permute-start | bytes 36872 | tf_op jit(solution)/shard_map/ppermute | solution.py:474
  23.9 7.1 %collective-permute-start.9 = (bf16[96,1024]{1,0:T(8,128)(2,1)S(1)}, bf16[96,1024]{1,0:T(8,128)(2,1)S(1)}, u32[]{:S(2)}, u32[]{:S(2)}) collective-permute-start(bf16[96,1024]{1,0:T(8,128)(2,1)S(1)} %pad_maximum_fusion.9), channel_id=1, source_target_pairs={{0,4},{1,3},{2,6},{3,1},{4,0},{5,7},{6,2},{7,5},{8,12},{9,11},{10,... | collective-permute-start | bytes 589832 | tf_op jit(solution)/shard_map/ppermute | solution.py:559
  26.2 8.2 %collective-permute-start.10 = (bf16[48,2432]{1,0:T(8,128)(2,1)S(1)}, bf16[48,2432]{1,0:T(8,128)(2,1)S(1)}, u32[]{:S(2)}, u32[]{:S(2)}) collective-permute-start(bf16[48,2432]{1,0:T(8,128)(2,1)S(1)} %pad_maximum_fusion.8), channel_id=1, source_target_pairs={{0,8},{1,17},{2,10},{3,19},{4,12},{5,21},{6,14},{7,23},{8,0},{9,25... | collective-permute-start | bytes 700424 | tf_op jit(solution)/shard_map/ppermute | solution.py:559
  26.3 8.9 %collective-permute-start.8 = (bf16[192,1280]{1,0:T(8,128)(2,1)S(1)}, bf16[192,1280]{1,0:T(8,128)(2,1)S(1)}, u32[]{:S(2)}, u32[]{:S(2)}) collective-permute-start(bf16[192,1280]{1,0:T(8,128)(2,1)S(1)} %pad_maximum_fusion.4), channel_id=1, source_target_pairs={{0,2},{1,5},{2,0},{3,7},{4,6},{5,1},{6,4},{7,3},{8,10},{9,13},{10,... | collective-permute-start | bytes 1474568 | tf_op jit(solution)/shard_map/ppermute | solution.py:559
  35.3 15.0 %collective-permute-start.13 = (bf16[384,1280]{1,0:T(8,128)(2,1)S(1)}, bf16[384,1280]{1,0:T(8,128)(2,1)S(1)}, u32[]{:S(2)}, u32[]{:S(2)}) collective-permute-start(bf16[384,1280]{1,0:T(8,128)(2,1)S(1)} %pad_maximum_fusion.1.refs_0_), channel_id=1, source_target_pairs={{0,1},{1,0},{2,3},{3,2},{4,5},{5,4},{6,7},{7,6},{8,9},{9,8},{10,11... | collective-permute-start | bytes 2949128 | tf_op jit(solution)/shard_map/ppermute | solution.py:474
  35.4 15.0 %collective-permute-start.12 = (bf16[384,1280]{1,0:T(8,128)(2,1)S(1)}, bf16[384,1280]{1,0:T(8,128)(2,1)S(1)}, u32[]{:S(2)}, u32[]{:S(2)}) collective-permute-start(bf16[384,1280]{1,0:T(8,128)(2,1)S(1)} %pad_maximum_fusion.1.refs_0_), channel_id=1, source_target_pairs={{0,4},{1,3},{2,6},{3,1},{4,0},{5,7},{6,2},{7,5},{8,12},{9,11},{10,... | collective-permute-start | bytes 2949128 | tf_op jit(solution)/shard_map/ppermute | solution.py:559
  36.2 14.1 %collective-permute-start.11 = (bf16[96,2432]{1,0:T(8,128)(2,1)S(1)}, bf16[96,2432]{1,0:T(8,128)(2,1)S(1)}, u32[]{:S(2)}, u32[]{:S(2)}) collective-permute-start(bf16[96,2432]{1,0:T(8,128)(2,1)S(1)} %pad_maximum_fusion.5), channel_id=1, source_target_pairs={{0,16},{1,9},{2,18},{3,11},{4,20},{5,13},{6,22},{7,15},{8,24},{9,1... | collective-permute-start | bytes 1400840 | tf_op jit(solution)/shard_map/ppermute | solution.py:559
  50.4 13.6 %collective-permute-start.15 = (bf16[192,2432]{1,0:T(8,128)(2,1)S(1)}, bf16[192,2432]{1,0:T(8,128)(2,1)S(1)}, u32[]{:S(2)}, u32[]{:S(2)}) collective-permute-start(bf16[192,2432]{1,0:T(8,128)(2,1)S(1)} %pad_maximum_fusion.2), channel_id=1, source_target_pairs={{0,2},{1,5},{2,0},{3,7},{4,6},{5,1},{6,4},{7,3},{8,10},{9,13},{10,... | collective-permute-start | bytes 2801672 | tf_op jit(solution)/shard_map/ppermute | solution.py:559
  52.1 12.1 %collective-permute-start.16 = (bf16[384,1280]{1,0:T(8,128)(2,1)S(1)}, bf16[384,1280]{1,0:T(8,128)(2,1)S(1)}, u32[]{:S(2)}, u32[]{:S(2)}) collective-permute-start(bf16[384,1280]{1,0:T(8,128)(2,1)S(1)} %collective-permute-done.12.refs_1_), channel_id=1, source_target_pairs={{0,1},{1,0},{2,3},{3,2},{4,5},{5,4},{6,7},{7,6},{8,9},{9,8},{10,11... | collective-permute-start | bytes 2949128 | tf_op jit(solution)/shard_map/ppermute | solution.py:474
  52.1 11.0 %collective-permute-start.14 = (bf16[192,1024]{1,0:T(8,128)(2,1)S(1)}, bf16[192,1024]{1,0:T(8,128)(2,1)S(1)}, u32[]{:S(2)}, u32[]{:S(2)}) collective-permute-start(bf16[192,1024]{1,0:T(8,128)(2,1)S(1)} %pad_maximum_fusion.6), channel_id=1, source_target_pairs={{0,8},{1,17},{2,10},{3,19},{4,12},{5,21},{6,14},{7,23},{8,0},{9,25... | collective-permute-start | bytes 1179656 | tf_op jit(solution)/shard_map/ppermute | solution.py:559
  65.2 25.7 %collective-permute-start.17 = (bf16[384,2432]{1,0:T(8,128)(2,1)S(1)}, bf16[384,2432]{1,0:T(8,128)(2,1)}, u32[]{:S(2)}, u32[]{:S(2)}) collective-permute-start(bf16[384,2432]{1,0:T(8,128)(2,1)S(1)} %pad_maximum_fusion.refs_0_), channel_id=1, source_target_pairs={{0,4},{1,3},{2,6},{3,1},{4,0},{5,7},{6,2},{7,5},{8,12},{9,11},{10,... | collective-permute-start | bytes 5603336 | tf_op jit(solution)/shard_map/ppermute | solution.py:559
  66.5 29.7 %collective-permute-start.19 = (bf16[384,2432]{1,0:T(8,128)(2,1)S(1)}, bf16[384,2432]{1,0:T(8,128)(2,1)}, u32[]{:S(2)}, u32[]{:S(2)}) collective-permute-start(bf16[384,2432]{1,0:T(8,128)(2,1)S(1)} %pad_maximum_fusion.refs_0_), channel_id=1, source_target_pairs={{0,1},{1,0},{2,3},{3,2},{4,5},{5,4},{6,7},{7,6},{8,9},{9,8},{10,11... | collective-permute-start | bytes 5603336 | tf_op jit(solution)/shard_map/ppermute | solution.py:474
  66.5 24.4 %collective-permute-start.18 = (bf16[384,1024]{1,0:T(8,128)(2,1)S(1)}, bf16[384,1024]{1,0:T(8,128)(2,1)S(1)}, u32[]{:S(2)}, u32[]{:S(2)}) collective-permute-start(bf16[384,1024]{1,0:T(8,128)(2,1)S(1)} %pad_maximum_fusion.3.refs_4_), channel_id=1, source_target_pairs={{0,16},{1,9},{2,18},{3,11},{4,20},{5,13},{6,22},{7,15},{8,24},{9,1... | collective-permute-start | bytes 2359304 | tf_op jit(solution)/shard_map/ppermute | solution.py:559
  90.9 6.4 %collective-permute-start.20 = (bf16[384,2432]{1,0:T(8,128)(2,1)}, bf16[384,2432]{1,0:T(8,128)(2,1)}, u32[]{:S(2)}, u32[]{:S(2)}) collective-permute-start(bf16[384,2432]{1,0:T(8,128)(2,1)} %collective-permute-done.17.refs_1_), channel_id=1, source_target_pairs={{0,1},{1,0},{2,3},{3,2},{4,5},{5,4},{6,7},{7,6},{8,9},{9,8},{10,11... | collective-permute-start | bytes 5603336 | tf_op jit(solution)/shard_map/ppermute | solution.py:474
  91.5 5.8 %collective-permute-start.22 = (bf16[384,1024]{1,0:T(8,128)(2,1)S(1)}, bf16[384,1024]{1,0:T(8,128)(2,1)S(1)}, u32[]{:S(2)}, u32[]{:S(2)}) collective-permute-start(bf16[384,1024]{1,0:T(8,128)(2,1)S(1)} %collective-permute-done.18.refs_5_), channel_id=1, source_target_pairs={{0,1},{1,0},{2,3},{3,2},{4,5},{5,4},{6,7},{7,6},{8,9},{9,8},{10,11... | collective-permute-start | bytes 2359304 | tf_op jit(solution)/shard_map/ppermute | solution.py:474
  160.7 16.5 %collective-permute-start.25 = (f32[16,768]{1,0:T(8,128)}, f32[16,768]{1,0:T(8,128)S(1)}, u32[]{:S(2)}, u32[]{:S(2)}) collective-permute-start(f32[16,768]{1,0:T(8,128)} %get-tuple-element.86), channel_id=1, source_target_pairs={{0,24},{2,26},{4,28},{6,30},{8,16},{10,18},{12,20},{14,22},{16,8},... | collective-permute-start | bytes 147464 | tf_op jit(solution)/shard_map/ppermute | solution.py:482
  162.4 14.8 %collective-permute-start.24 = (f32[16,768]{1,0:T(8,128)}, f32[16,768]{1,0:T(8,128)S(1)}, u32[]{:S(2)}, u32[]{:S(2)}) collective-permute-start(f32[16,768]{1,0:T(8,128)} %get-tuple-element.86), channel_id=1, source_target_pairs={{0,16},{2,18},{4,20},{6,22},{8,24},{10,26},{12,28},{14,30},{16,0},... | collective-permute-start | bytes 147464 | tf_op jit(solution)/shard_map/ppermute | solution.py:482
  163.8 13.4 %collective-permute-start.23 = (f32[16,768]{1,0:T(8,128)}, f32[16,768]{1,0:T(8,128)S(1)}, u32[]{:S(2)}, u32[]{:S(2)}) collective-permute-start(f32[16,768]{1,0:T(8,128)} %get-tuple-element.86), channel_id=1, source_target_pairs={{0,8},{2,10},{4,12},{6,14},{8,0},{10,2},{12,4},{14,6},{16,24},{18,... | collective-permute-start | bytes 147464 | tf_op jit(solution)/shard_map/ppermute | solution.py:482
  (35 other events, 319.6 us)
where the time goes:
time: 187 us; the launch traced here: 186 us
  Pallas kernels  96.4 us (52%)
  waiting for transfers between devices  43.6 us (23%)
  starting transfers between devices  29.6 us (16%)
  local copies, waits for them, and re-layouts  8.31 us (4%)
  other arithmetic  6.86 us (4%)
    pallas_call x4, Pallas kernels, call(): pl.pallas_call(kernel, grid_spec=pltpu.PrefetchScalarGridSpec(num_scalar_...  96.4 us
    ppermute x12, waiting for transfers between devices, exchange(): return lax.ppermute(array, ('dp', 'tensor'), pairs)  37.3 us
    ppermute x12, starting transfers between devices, exchange(): return lax.ppermute(array, ('dp', 'tensor'), pairs)  18.8 us
    ppermute x6, starting transfers between devices, over_dp(): return lax.ppermute(array, 'dp', [(i, target(i)) for i in range(count)])  7.94 us
    ppermute x14, waiting for transfers between devices, swap(): return lax.ppermute(array, 'tensor', [(0, 1), (1, 0)])  5.58 us
  transfers between devices with their start and end apart: 32, of which 14 were waited for; matrix products, arithmetic and copies ran while one was open for 7% of the time, Pallas kernels for 18%

commit v1 on v0

--- a/solution.py
+++ b/solution.py
@@ -523,9 +523,9 @@
     last = hidden // 3 if count == 16 else hidden // 2
     first = hidden - last
 
-    down = jnp.transpose(adapter_down_weight, (1, 0, 2)).reshape(shard_rows, 2 * RANK)
-    down = jnp.pad(down, ((0, 0), (0, LANES - 2 * RANK)))
-    shard = jnp.concatenate([query_matrix, key_matrix, value_matrix, down], axis=1)
+    blank = jnp.zeros((shard_rows, LANES - 2 * RANK), BF16)
+    down = [adapter_down_weight[0], adapter_down_weight[1], blank]
+    shard = jnp.concatenate([query_matrix, key_matrix, value_matrix, *down], axis=1)
     back = feedforward_output_weight.T
     shard_first = jnp.concatenate(
         [attention_output_weight.T, feedforward_input_weight[:, :first], back[:, :first]], axis=1
@@ -561,17 +561,17 @@
         def joined(*arrays):
             return jnp.concatenate(arrays, axis=0)
 
+        shard, shard_last = lax.optimization_barrier((shard, after(shard_last, shard)))
         line = joined(shard, exchange(shard, LINE_FIRST, 0))
-        line, shard_last = lax.optimization_barrier((line, shard_last))
         plane = joined(shard_last, exchange(shard_last, PLANE_FIRST, 0))
         line = joined(line, exchange(line, LINE_FIRST, 1))
+        plane = joined(plane, exchange(plane, PLANE_FIRST, 1))
         line, plane, *early = lax.optimization_barrier((line, plane, x_got, up_got, grad_got, hidden_bias_got, offsets, bias))
         x_got, up_got, grad_got, hidden_bias_got, offsets, bias = early
         shard_first = after(shard_first, line)
         line_first = joined(shard_first, exchange(shard_first, LINE_FIRST, 0))
-        plane = joined(plane, exchange(plane, PLANE_FIRST, 1))
         line = joined(line, exchange(line, LINE_FIRST, 2))
-        line, plane, line_first = lax.optimization_barrier((line, plane, line_first))
+        line_first = after(line_first, line)
         line_first = joined(line_first, exchange(line_first, LINE_FIRST, 1))
         own = [line, exchange(line, LINE_FIRST, 3)]
         swapped = [swap(line)]
@@ -579,7 +579,7 @@
         swapped.append(swap(own[1]))
         line_first = joined(line_first, exchange(line_first, LINE_FIRST, 2))
         plane = joined(plane, exchange(plane, PLANE_FIRST, 2))
-        plane, line_first, x_got, swapped = lax.optimization_barrier((plane, line_first, x_got, swapped))
+        plane, line_first, x_got = lax.optimization_barrier((plane, line_first, x_got))
         own_first = [line_first, exchange(line_first, LINE_FIRST, 3)]
         own_last = [plane, exchange(plane, PLANE_FIRST, 3)]
         got_first, got_last = [swap(line_first)], [swap(plane)]

time: 187 us -> 182 us (0.973)
  other arithmetic: 6.86 us -> 2.92 us
  transfers between devices with their start and end apart: 32 -> 32, of which waited for: 14 -> 12; matrix products, arithmetic and copies ran while one was open for 7% -> 5% of each run, Pallas kernels for 18% -> 19%
where the time goes in v1:
time: 182 us
  Pallas kernels  96.3 us (53%)
  waiting for transfers between devices  43.7 us (24%)
  starting transfers between devices  28.9 us (16%)
  local copies, waits for them, and re-layouts  8.77 us (5%)
  other arithmetic  2.92 us (2%)
    pallas_call x4, Pallas kernels, call(): pl.pallas_call(kernel, grid_spec=pltpu.PrefetchScalarGridSpec(num_scalar_...  96.3 us
    ppermute x12, waiting for transfers between devices, exchange(): return lax.ppermute(array, ('dp', 'tensor'), pairs)  37 us
    ppermute x12, starting transfers between devices, exchange(): return lax.ppermute(array, ('dp', 'tensor'), pairs)  17.6 us
    ppermute x6, starting transfers between devices, over_dp(): return lax.ppermute(array, 'dp', [(i, target(i)) for i in range(count)])  8.01 us
    ppermute x14, waiting for transfers between devices, swap(): return lax.ppermute(array, 'tensor', [(0, 1), (1, 0)])  5.74 us
  transfers between devices with their start and end apart: 32, of which 12 were waited for; matrix products, arithmetic and copies ran while one was open for 5% of the time, Pallas kernels for 19%

profile of v1, /device:TPU:0, one launch (start us, length us, event | category | flops | bytes accessed | tf_op | source)
XLA Modules:
  0.0 181.8 jit_solution(15298379293583770150)
XLA Ops:
  4.7 3.0 %collective-permute-start.2 = (bf16[48,1024]{1,0:T(8,128)(2,1)S(1)}, bf16[48,1024]{1,0:T(8,128)(2,1)S(1)}, u32[]{:S(2)}, u32[]{:S(2)}) collective-permute-start(bf16[48,1024]{1,0:T(8,128)(2,1)S(1)} %pad_maximum_fusion.9), channel_id=1, source_target_pairs={{0,2},{1,5},{2,0},{3,7},{4,6},{5,1},{6,4},{7,3},{8,10},{9,13},{10,... | collective-permute-start | bytes 294920 | tf_op jit(solution)/shard_map/ppermute | solution.py:559
  7.7 1.6 collective-permute-start
  9.3 1.2 constant_dynamic-slice_fusion.1
  12.2 1.5 collective-permute-start.3
  13.7 2.7 %collective-permute-start.1 = (bf16[96,1280]{1,0:T(8,128)(2,1)S(1)}, bf16[96,1280]{1,0:T(8,128)(2,1)S(1)}, u32[]{:S(2)}, u32[]{:S(2)}) collective-permute-start(bf16[96,1280]{1,0:T(8,128)(2,1)S(1)} %pad_maximum_fusion.6), channel_id=1, source_target_pairs={{0,16},{1,9},{2,18},{3,11},{4,20},{5,13},{6,22},{7,15},{8,24},{9,1... | collective-permute-start | bytes 737288 | tf_op jit(solution)/shard_map/ppermute | solution.py:559
  18.0 5.6 %collective-permute-done.1 = bf16[96,1280]{1,0:T(8,128)(2,1)S(1)} collective-permute-done((bf16[96,1280]{1,0:T(8,128)(2,1)S(1)}, bf16[96,1280]{1,0:T(8,128)(2,1)S(1)}, u32[]{:S(2)}, u32[]{:S(2)}) %collective-permute-start.1) | collective-permute-done | bytes 245792 | tf_op jit(solution)/shard_map/ppermute | solution.py:559
  23.8 1.8 collective-permute-start.9
  25.6 7.0 %collective-permute-done.10 = bf16[192,1280]{1,0:T(8,128)(2,1)S(1)} collective-permute-done((bf16[192,1280]{1,0:T(8,128)(2,1)S(1)}, bf16[192,1280]{1,0:T(8,128)(2,1)S(1)}, u32[]{:S(2)}, u32[]{:S(2)}) %collective-permute-start.10) | collective-permute-done | bytes 491552 | tf_op jit(solution)/shard_map/ppermute | solution.py:559
  34.3 12.6 %collective-permute-done.11 = bf16[96,2432]{1,0:T(8,128)(2,1)S(1)} collective-permute-done((bf16[96,2432]{1,0:T(8,128)(2,1)S(1)}, bf16[96,2432]{1,0:T(8,128)(2,1)S(1)}, u32[]{:S(2)}, u32[]{:S(2)}) %collective-permute-start.11) | collective-permute-done | bytes 466976 | tf_op jit(solution)/shard_map/ppermute | solution.py:559
  47.0 2.6 %collective-permute-start.16 = (bf16[192,2432]{1,0:T(8,128)(2,1)S(1)}, bf16[192,2432]{1,0:T(8,128)(2,1)S(1)}, u32[]{:S(2)}, u32[]{:S(2)}) collective-permute-start(bf16[192,2432]{1,0:T(8,128)(2,1)S(1)} %pad_maximum_fusion.1), channel_id=1, source_target_pairs={{0,2},{1,5},{2,0},{3,7},{4,6},{5,1},{6,4},{7,3},{8,10},{9,13},{10,... | collective-permute-start | bytes 2801672 | tf_op jit(solution)/shard_map/ppermute | solution.py:559
  50.2 10.1 %collective-permute-done.15 = bf16[192,1024]{1,0:T(8,128)(2,1)S(1)} collective-permute-done((bf16[192,1024]{1,0:T(8,128)(2,1)S(1)}, bf16[192,1024]{1,0:T(8,128)(2,1)S(1)}, u32[]{:S(2)}, u32[]{:S(2)}) %collective-permute-start.15) | collective-permute-done | bytes 393248 | tf_op jit(solution)/shard_map/ppermute | solution.py:559
  61.3 2.3 %collective-permute-start.17 = (bf16[384,2432]{1,0:T(8,128)(2,1)S(1)}, bf16[384,2432]{1,0:T(8,128)(2,1)}, u32[]{:S(2)}, u32[]{:S(2)}) collective-permute-start(bf16[384,2432]{1,0:T(8,128)(2,1)S(1)} %pad_maximum_fusion.refs_0_), channel_id=1, source_target_pairs={{0,4},{1,3},{2,6},{3,1},{4,0},{5,7},{6,2},{7,5},{8,12},{9,11},{10,... | collective-permute-start | bytes 5603336 | tf_op jit(solution)/shard_map/ppermute | solution.py:559
  64.3 21.7 %project_attend.1 = (bf16[2,512,2304]{2,1,0:T(8,128)(2,1)}, bf16[2,512,768]{2,1,0:T(8,128)(2,1)}, bf16[2,512,128]{2,1,0:T(8,128)(2,1)}, bf16[2,512,256]{2,1,0:T(8,128)(2,1)}) custom-call(s32[64]{0:T(128)} %pad_add_fusion.offsets, s32[2]{0:T(128)} %get-tuple-element.107.lengths, s32[2]{0:T(128)} %get-tuple-element.108.bounds, s32[1]{0:T(128)} %bitcast.2.core_ref, ...), custom_call_target="tpu_custom_call" | custom-call | flops 11274289152 | bytes 9437184 | tf_op jit(solution)/shard_map/project_attend/pallas_call | solution.py:457
  87.9 3.7 %collective-permute-done.21.refs_6_ = bf16[384,1024]{1,0:T(8,128)(2,1)S(1)} collective-permute-done((bf16[384,1024]{1,0:T(8,128)(2,1)S(1)}, bf16[384,1024]{1,0:T(8,128)(2,1)S(1)}, u32[]{:S(2)}, u32[]{:S(2)}) %collective-permute-start.21) | collective-permute-done | bytes 786464 | tf_op jit(solution)/shard_map/ppermute | solution.py:474
  93.6 36.4 %feed.1 = (bf16[4,256,768]{2,1,0:T(8,128)(2,1)}, bf16[2,256,768]{2,1,0:T(8,128)(2,1)}, f32[2,512,768]{2,1,0:T(8,128)}, bf16[2,512,768]{2,1,0:T(8,128)(2,1)}) custom-call(s32[64]{0:T(128)} %pad_add_fusion.offsets, s32[1]{0:T(128)} %bitcast.2.core_ref, bf16[384,2432]{1,0:T(8,128)(2,1)} %copy-done, bf16[384,2432]{1,0:T(8,128)(2,1)} %collective-permute-done.17.refs_1_, ...), custom_call_target="tpu_custom_call" | custom-call | flops 21743271936 | bytes 9437184 | tf_op jit(solution)/shard_map/feed/pallas_call | solution.py:457
  130.0 26.1 %attend_back.1 = (bf16[2,512,2304]{2,1,0:T(8,128)(2,1)}, f32[16,768]{1,0:T(8,128)}) custom-call(s32[2]{0:T(128)} %get-tuple-element.107.lengths, s32[2]{0:T(128)} %get-tuple-element.108.bounds, s32[1]{0:T(128)} %bitcast.2.core_ref, bf16[2,512,2304]{2,1,0:T(8,128)(2,1)} %get-tuple-element.67.refs_0_, bf16[2,512,768]{2,1,0:T(8,128)(2,1)} %get-tuple-element.68.refs_10_.refs_1_, ...), custom_call_target="tpu_custom_call" | custom-call | flops 16106127360 | bytes 12582912 | tf_op jit(solution)/shard_map/attend_back/pallas_call | solution.py:457
  156.1 2.6 %collective-permute-start.25 = (f32[16,768]{1,0:T(8,128)}, f32[16,768]{1,0:T(8,128)S(1)}, u32[]{:S(2)}, u32[]{:S(2)}) collective-permute-start(f32[16,768]{1,0:T(8,128)} %get-tuple-element.80), channel_id=1, source_target_pairs={{0,24},{2,26},{4,28},{6,30},{8,16},{10,18},{12,20},{14,22},{16,8},... | collective-permute-start | bytes 147464 | tf_op jit(solution)/shard_map/ppermute | solution.py:482
  158.6 1.9 %collective-permute-start.24 = (f32[16,768]{1,0:T(8,128)}, f32[16,768]{1,0:T(8,128)S(1)}, u32[]{:S(2)}, u32[]{:S(2)}) collective-permute-start(f32[16,768]{1,0:T(8,128)} %get-tuple-element.80), channel_id=1, source_target_pairs={{0,16},{2,18},{4,20},{6,22},{8,24},{10,26},{12,28},{14,30},{16,0},... | collective-permute-start | bytes 147464 | tf_op jit(solution)/shard_map/ppermute | solution.py:482
  160.5 12.1 %input_grad.1 = (f32[4,256,768]{2,1,0:T(8,128)}, f32[2,256,768]{2,1,0:T(8,128)}) custom-call(s32[64]{0:T(128)} %pad_add_fusion.offsets, s32[1]{0:T(128)} %bitcast.2.core_ref, bf16[384,1280]{1,0:T(8,128)(2,1)} %copy-done.3, bf16[384,1280]{1,0:T(8,128)(2,1)} %collective-permute-done.12.refs_1_, bf16[384,1280]{1,0:T(8,128)(2,1)} %copy-done.14, ...), custom_call_target="tpu_custom_call" | custom-call | flops 3623878656 | bytes 9437184 | tf_op jit(solution)/shard_map/input_grad/pallas_call | solution.py:457
  173.2 1.5 collective-permute-start.28
  174.7 1.1 collective-permute-start.27
  175.8 1.0 collective-permute-start.26
  177.5 1.3 constant_dynamic-update-slice_fusion.9
  180.0 1.2 collective-permute-done.31
  (136 shorter events, 18.2 us)
Async XLA Ops:
  0.7 11.3 %collective-permute-start.8 = (f32[2,384]{1,0:T(2,128)}, f32[2,384]{1,0:T(2,128)S(1)}, u32[]{:S(2)}, u32[]{:S(2)}) collective-permute-start(f32[2,384]{1,0:T(2,128)} %param.23), channel_id=1, source_target_pairs={{0,1},{1,0},{2,3},{3,2},{4,5},{5,4},{6,7},{7,6},{8,9},{9,8},{10,11... | collective-permute-start | bytes 9224 | tf_op jit(solution)/shard_map/ppermute | solution.py:474
  1.2 22.4 %collective-permute-start.7 = (f32[1536]{0:T(1024)}, f32[1536]{0:T(1024)S(1)}, u32[]{:S(2)}, u32[]{:S(2)}) collective-permute-start(f32[1536]{0:T(1024)} %param.28), channel_id=1, source_target_pairs={{0,1},{1,0},{2,3},{3,2},{4,5},{5,4},{6,7},{7,6},{8,9},{9,8},{10,11... | collective-permute-start | bytes 18440 | tf_op jit(solution)/shard_map/ppermute | solution.py:474
  4.7 7.4 %collective-permute-start.2 = (bf16[48,1024]{1,0:T(8,128)(2,1)S(1)}, bf16[48,1024]{1,0:T(8,128)(2,1)S(1)}, u32[]{:S(2)}, u32[]{:S(2)}) collective-permute-start(bf16[48,1024]{1,0:T(8,128)(2,1)S(1)} %pad_maximum_fusion.9), channel_id=1, source_target_pairs={{0,2},{1,5},{2,0},{3,7},{4,6},{5,1},{6,4},{7,3},{8,10},{9,13},{10,... | collective-permute-start | bytes 294920 | tf_op jit(solution)/shard_map/ppermute | solution.py:559
  7.7 6.0 %collective-permute-start = (bf16[48,1280]{1,0:T(8,128)(2,1)S(1)}, bf16[48,1280]{1,0:T(8,128)(2,1)S(1)}, u32[]{:S(2)}, u32[]{:S(2)}) collective-permute-start(bf16[48,1280]{1,0:T(8,128)(2,1)S(1)} %concatenate.47), channel_id=1, source_target_pairs={{0,8},{1,17},{2,10},{3,19},{4,12},{5,21},{6,14},{7,23},{8,0},{9,25... | collective-permute-start | bytes 368648 | tf_op jit(solution)/shard_map/ppermute | solution.py:559
  10.5 13.1 %collective-permute-start.4 = (bf16[2,256,768]{2,1,0:T(8,128)(2,1)S(1)}, bf16[2,256,768]{2,1,0:T(8,128)(2,1)}, u32[]{:S(2)}, u32[]{:S(2)}) collective-permute-start(bf16[2,256,768]{2,1,0:T(8,128)(2,1)S(1)} %constant_dynamic-slice_fusion.1), channel_id=1, source_target_pairs={{0,1},{1,0},{2,3},{3,2},{4,5},{5,4},{6,7},{7,6},{8,9},{9,8},{10,11... | collective-permute-start | bytes 2359304 | tf_op jit(solution)/shard_map/ppermute | solution.py:474
  12.0 11.7 %collective-permute-start.6 = (bf16[2,256,768]{2,1,0:T(8,128)(2,1)S(1)}, bf16[2,256,768]{2,1,0:T(8,128)(2,1)S(1)}, u32[]{:S(2)}, u32[]{:S(2)}) collective-permute-start(bf16[2,256,768]{2,1,0:T(8,128)(2,1)S(1)} %constant_dynamic-slice_fusion), channel_id=1, source_target_pairs={{0,1},{1,0},{2,3},{3,2},{4,5},{5,4},{6,7},{7,6},{8,9},{9,8},{10,11... | collective-permute-start | bytes 2359304 | tf_op jit(solution)/shard_map/ppermute | solution.py:474
  12.2 5.7 %collective-permute-start.3 = (bf16[96,1024]{1,0:T(8,128)(2,1)S(1)}, bf16[96,1024]{1,0:T(8,128)(2,1)S(1)}, u32[]{:S(2)}, u32[]{:S(2)}) collective-permute-start(bf16[96,1024]{1,0:T(8,128)(2,1)S(1)} %pad_maximum_fusion.8), channel_id=1, source_target_pairs={{0,4},{1,3},{2,6},{3,1},{4,0},{5,7},{6,2},{7,5},{8,12},{9,11},{10,... | collective-permute-start | bytes 589832 | tf_op jit(solution)/shard_map/ppermute | solution.py:559
  13.7 9.8 %collective-permute-start.1 = (bf16[96,1280]{1,0:T(8,128)(2,1)S(1)}, bf16[96,1280]{1,0:T(8,128)(2,1)S(1)}, u32[]{:S(2)}, u32[]{:S(2)}) collective-permute-start(bf16[96,1280]{1,0:T(8,128)(2,1)S(1)} %pad_maximum_fusion.6), channel_id=1, source_target_pairs={{0,16},{1,9},{2,18},{3,11},{4,20},{5,13},{6,22},{7,15},{8,24},{9,1... | collective-permute-start | bytes 737288 | tf_op jit(solution)/shard_map/ppermute | solution.py:559
  23.7 8.9 %collective-permute-start.10 = (bf16[192,1280]{1,0:T(8,128)(2,1)S(1)}, bf16[192,1280]{1,0:T(8,128)(2,1)S(1)}, u32[]{:S(2)}, u32[]{:S(2)}) collective-permute-start(bf16[192,1280]{1,0:T(8,128)(2,1)S(1)} %pad_maximum_fusion.3), channel_id=1, source_target_pairs={{0,2},{1,5},{2,0},{3,7},{4,6},{5,1},{6,4},{7,3},{8,10},{9,13},{10,... | collective-permute-start | bytes 1474568 | tf_op jit(solution)/shard_map/ppermute | solution.py:559
  23.8 9.6 %collective-permute-start.9 = (bf16[48,2432]{1,0:T(8,128)(2,1)S(1)}, bf16[48,2432]{1,0:T(8,128)(2,1)S(1)}, u32[]{:S(2)}, u32[]{:S(2)}) collective-permute-start(bf16[48,2432]{1,0:T(8,128)(2,1)S(1)} %pad_maximum_fusion.7), channel_id=1, source_target_pairs={{0,8},{1,17},{2,10},{3,19},{4,12},{5,21},{6,14},{7,23},{8,0},{9,25... | collective-permute-start | bytes 700424 | tf_op jit(solution)/shard_map/ppermute | solution.py:559
  32.6 14.3 %collective-permute-start.13 = (bf16[384,1280]{1,0:T(8,128)(2,1)S(1)}, bf16[384,1280]{1,0:T(8,128)(2,1)S(1)}, u32[]{:S(2)}, u32[]{:S(2)}) collective-permute-start(bf16[384,1280]{1,0:T(8,128)(2,1)S(1)} %constant_dynamic-update-slice_fusion.1.refs_0_), channel_id=1, source_target_pairs={{0,1},{1,0},{2,3},{3,2},{4,5},{5,4},{6,7},{7,6},{8,9},{9,8},{10,11... | collective-permute-start | bytes 2949128 | tf_op jit(solution)/shard_map/ppermute | solution.py:474
  32.7 14.3 %collective-permute-start.12 = (bf16[384,1280]{1,0:T(8,128)(2,1)S(1)}, bf16[384,1280]{1,0:T(8,128)(2,1)}, u32[]{:S(2)}, u32[]{:S(2)}) collective-permute-start(bf16[384,1280]{1,0:T(8,128)(2,1)S(1)} %constant_dynamic-update-slice_fusion.1.refs_0_), channel_id=1, source_target_pairs={{0,4},{1,3},{2,6},{3,1},{4,0},{5,7},{6,2},{7,5},{8,12},{9,11},{10,... | collective-permute-start | bytes 2949128 | tf_op jit(solution)/shard_map/ppermute | solution.py:559
  33.4 13.5 %collective-permute-start.11 = (bf16[96,2432]{1,0:T(8,128)(2,1)S(1)}, bf16[96,2432]{1,0:T(8,128)(2,1)S(1)}, u32[]{:S(2)}, u32[]{:S(2)}) collective-permute-start(bf16[96,2432]{1,0:T(8,128)(2,1)S(1)} %pad_maximum_fusion.4), channel_id=1, source_target_pairs={{0,16},{1,9},{2,18},{3,11},{4,20},{5,13},{6,22},{7,15},{8,24},{9,1... | collective-permute-start | bytes 1400840 | tf_op jit(solution)/shard_map/ppermute | solution.py:559
  47.0 14.2 %collective-permute-start.16 = (bf16[192,2432]{1,0:T(8,128)(2,1)S(1)}, bf16[192,2432]{1,0:T(8,128)(2,1)S(1)}, u32[]{:S(2)}, u32[]{:S(2)}) collective-permute-start(bf16[192,2432]{1,0:T(8,128)(2,1)S(1)} %pad_maximum_fusion.1), channel_id=1, source_target_pairs={{0,2},{1,5},{2,0},{3,7},{4,6},{5,1},{6,4},{7,3},{8,10},{9,13},{10,... | collective-permute-start | bytes 2801672 | tf_op jit(solution)/shard_map/ppermute | solution.py:559
  49.6 10.7 %collective-permute-start.15 = (bf16[192,1024]{1,0:T(8,128)(2,1)S(1)}, bf16[192,1024]{1,0:T(8,128)(2,1)S(1)}, u32[]{:S(2)}, u32[]{:S(2)}) collective-permute-start(bf16[192,1024]{1,0:T(8,128)(2,1)S(1)} %pad_maximum_fusion.5), channel_id=1, source_target_pairs={{0,8},{1,17},{2,10},{3,19},{4,12},{5,21},{6,14},{7,23},{8,0},{9,25... | collective-permute-start | bytes 1179656 | tf_op jit(solution)/shard_map/ppermute | solution.py:559
  50.2 14.1 %collective-permute-start.14 = (bf16[384,1280]{1,0:T(8,128)(2,1)}, bf16[384,1280]{1,0:T(8,128)(2,1)}, u32[]{:S(2)}, u32[]{:S(2)}) collective-permute-start(bf16[384,1280]{1,0:T(8,128)(2,1)} %collective-permute-done.12.refs_1_), channel_id=1, source_target_pairs={{0,1},{1,0},{2,3},{3,2},{4,5},{5,4},{6,7},{7,6},{8,9},{9,8},{10,11... | collective-permute-start | bytes 2949128 | tf_op jit(solution)/shard_map/ppermute | solution.py:474
  61.3 24.7 %collective-permute-start.17 = (bf16[384,2432]{1,0:T(8,128)(2,1)S(1)}, bf16[384,2432]{1,0:T(8,128)(2,1)}, u32[]{:S(2)}, u32[]{:S(2)}) collective-permute-start(bf16[384,2432]{1,0:T(8,128)(2,1)S(1)} %pad_maximum_fusion.refs_0_), channel_id=1, source_target_pairs={{0,4},{1,3},{2,6},{3,1},{4,0},{5,7},{6,2},{7,5},{8,12},{9,11},{10,... | collective-permute-start | bytes 5603336 | tf_op jit(solution)/shard_map/ppermute | solution.py:559
  64.2 27.3 %collective-permute-start.19 = (bf16[384,2432]{1,0:T(8,128)(2,1)S(1)}, bf16[384,2432]{1,0:T(8,128)(2,1)}, u32[]{:S(2)}, u32[]{:S(2)}) collective-permute-start(bf16[384,2432]{1,0:T(8,128)(2,1)S(1)} %pad_maximum_fusion.refs_0_), channel_id=1, source_target_pairs={{0,1},{1,0},{2,3},{3,2},{4,5},{5,4},{6,7},{7,6},{8,9},{9,8},{10,11... | collective-permute-start | bytes 5603336 | tf_op jit(solution)/shard_map/ppermute | solution.py:474
  64.2 21.8 %collective-permute-start.18 = (bf16[384,1024]{1,0:T(8,128)(2,1)S(1)}, bf16[384,1024]{1,0:T(8,128)(2,1)}, u32[]{:S(2)}, u32[]{:S(2)}) collective-permute-start(bf16[384,1024]{1,0:T(8,128)(2,1)S(1)} %pad_maximum_fusion.2.refs_4_), channel_id=1, source_target_pairs={{0,16},{1,9},{2,18},{3,11},{4,20},{5,13},{6,22},{7,15},{8,24},{9,1... | collective-permute-start | bytes 2359304 | tf_op jit(solution)/shard_map/ppermute | solution.py:559
  86.0 7.5 %collective-permute-start.20 = (bf16[384,2432]{1,0:T(8,128)(2,1)}, bf16[384,2432]{1,0:T(8,128)(2,1)}, u32[]{:S(2)}, u32[]{:S(2)}) collective-permute-start(bf16[384,2432]{1,0:T(8,128)(2,1)} %collective-permute-done.17.refs_1_), channel_id=1, source_target_pairs={{0,1},{1,0},{2,3},{3,2},{4,5},{5,4},{6,7},{7,6},{8,9},{9,8},{10,11... | collective-permute-start | bytes 5603336 | tf_op jit(solution)/shard_map/ppermute | solution.py:474
  86.8 5.8 %collective-permute-start.22 = (bf16[384,1024]{1,0:T(8,128)(2,1)}, bf16[384,1024]{1,0:T(8,128)(2,1)S(1)}, u32[]{:S(2)}, u32[]{:S(2)}) collective-permute-start(bf16[384,1024]{1,0:T(8,128)(2,1)} %collective-permute-done.18.refs_5_), channel_id=1, source_target_pairs={{0,1},{1,0},{2,3},{3,2},{4,5},{5,4},{6,7},{7,6},{8,9},{9,8},{10,11... | collective-permute-start | bytes 2359304 | tf_op jit(solution)/shard_map/ppermute | solution.py:474
  156.1 16.5 %collective-permute-start.25 = (f32[16,768]{1,0:T(8,128)}, f32[16,768]{1,0:T(8,128)S(1)}, u32[]{:S(2)}, u32[]{:S(2)}) collective-permute-start(f32[16,768]{1,0:T(8,128)} %get-tuple-element.80), channel_id=1, source_target_pairs={{0,24},{2,26},{4,28},{6,30},{8,16},{10,18},{12,20},{14,22},{16,8},... | collective-permute-start | bytes 147464 | tf_op jit(solution)/shard_map/ppermute | solution.py:482
  158.6 14.0 %collective-permute-start.24 = (f32[16,768]{1,0:T(8,128)}, f32[16,768]{1,0:T(8,128)S(1)}, u32[]{:S(2)}, u32[]{:S(2)}) collective-permute-start(f32[16,768]{1,0:T(8,128)} %get-tuple-element.80), channel_id=1, source_target_pairs={{0,16},{2,18},{4,20},{6,22},{8,24},{10,26},{12,28},{14,30},{16,0},... | collective-permute-start | bytes 147464 | tf_op jit(solution)/shard_map/ppermute | solution.py:482
  160.5 12.1 %collective-permute-start.23 = (f32[16,768]{1,0:T(8,128)}, f32[16,768]{1,0:T(8,128)S(1)}, u32[]{:S(2)}, u32[]{:S(2)}) collective-permute-start(f32[16,768]{1,0:T(8,128)} %get-tuple-element.80), channel_id=1, source_target_pairs={{0,8},{2,10},{4,12},{6,14},{8,0},{10,2},{12,4},{14,6},{16,24},{18,... | collective-permute-start | bytes 147464 | tf_op jit(solution)/shard_map/ppermute | solution.py:482
  (30 other events, 306.4 us)

commit v2 on v1

--- a/solution.py
+++ b/solution.py
@@ -533,7 +533,8 @@
     shard_last = jnp.concatenate([feedforward_input_weight[:, first:], back[:, first:]], axis=1)
 
     others = (1 - core) * mine
-    x_got = swap(lax.dynamic_slice_in_dim(inputs, others, mine, 0))
+    x_send = lax.dynamic_slice_in_dim(inputs, others, mine, 0)
+    x_got = swap(x_send)
     grad_got = swap(lax.dynamic_slice_in_dim(output_gradient, others, mine, 0))
     bias_got, up_got, hidden_bias_got = map(swap, (query_value_bias, adapter_up_weight, feedforward_input_bias))
 
@@ -561,10 +562,11 @@
         def joined(*arrays):
             return jnp.concatenate(arrays, axis=0)
 
-        shard, shard_last = lax.optimization_barrier((shard, after(shard_last, shard)))
-        line = joined(shard, exchange(shard, LINE_FIRST, 0))
+        shard_last = after(shard_last, x_send)
+        line = line_start = joined(shard, exchange(shard, LINE_FIRST, 0))
         plane = joined(shard_last, exchange(shard_last, PLANE_FIRST, 0))
         line = joined(line, exchange(line, LINE_FIRST, 1))
+        plane = after(plane, line_start)
         plane = joined(plane, exchange(plane, PLANE_FIRST, 1))
         line, plane, *early = lax.optimization_barrier((line, plane, x_got, up_got, grad_got, hidden_bias_got, offsets, bias))
         x_got, up_got, grad_got, hidden_bias_got, offsets, bias = early
@@ -673,7 +675,7 @@
         4 * tokens * width * (width + 4 * hidden),
         8 * width * hidden,
     )
-    out_send = swap(out_send)
+    out_got = swap(out_send)
     adapter = (2 * RANK, width)
     grads, adapter = call(
         attend_back_kernel,
@@ -687,6 +689,7 @@
         2 * tokens * width * 20 * slot,
         16 * tokens * width,
     )
+    grads, out_got = lax.optimization_barrier((grads, out_got))
     if count == 16:
         ways = [over_dp(count, adapter, lambda i, flip=flip: i ^ flip) for flip in (4, 8, 12)]
     total, total_send = call(
@@ -710,13 +713,13 @@
         adapter = (adapter + ways[0]) + (ways[1] + ways[2])
         ways = [over_dp(count, adapter, lambda i, flip=flip: i ^ flip) for flip in (1, 2, 3)]
         input_grad = lax.dynamic_update_slice_in_dim(total, swap(total_send), others, 0)
-        result = lax.dynamic_update_slice_in_dim(out, out_send, others, 0)
+        result = lax.dynamic_update_slice_in_dim(out, out_got, others, 0)
         *ways, input_grad, result = lax.optimization_barrier((*ways, input_grad, result))
         adapter = (adapter + ways[0]) + (ways[1] + ways[2])
     else:
         adapter = lax.psum(adapter, "dp")
         input_grad = lax.dynamic_update_slice_in_dim(total, swap(total_send), others, 0)
-        result = lax.dynamic_update_slice_in_dim(out, out_send, others, 0)
+        result = lax.dynamic_update_slice_in_dim(out, out_got, others, 0)
     adapter = adapter[:, :heads] + swap(adapter[:, heads:])
     return result, input_grad, adapter.reshape(2, RANK, heads)
 

time: 182 us -> 181 us (level)
  waiting for transfers between devices: 43.7 us -> 48.3 us
  starting transfers between devices: 28.9 us -> 24.9 us
    ppermute x12, waiting for transfers between devices: 37 us -> 41 us  [exchange(): return lax.ppermute(array, ('dp', 'tensor'), pairs)]
    ppermute x12, starting transfers between devices: 17.6 us -> 14.4 us  [exchange(): return lax.ppermute(array, ('dp', 'tensor'), pairs)]
  transfers between devices with their start and end apart: 32 -> 32, of which waited for: 12 -> 13; matrix products, arithmetic and copies ran while one was open for 5% -> 4% of each run, Pallas kernels for 19% -> 33%
where the time goes in v2:
time: 181 us
  Pallas kernels  96.4 us (53%)
  waiting for transfers between devices  48.3 us (27%)
  starting transfers between devices  24.9 us (14%)
  local copies, waits for them, and re-layouts  7.1 us (4%)
  other arithmetic  2.96 us (2%)
    pallas_call x4, Pallas kernels, call(): pl.pallas_call(kernel, grid_spec=pltpu.PrefetchScalarGridSpec(num_scalar_...  96.4 us
    ppermute x12, waiting for transfers between devices, exchange(): return lax.ppermute(array, ('dp', 'tensor'), pairs)  41 us
    ppermute x12, starting transfers between devices, exchange(): return lax.ppermute(array, ('dp', 'tensor'), pairs)  14.4 us
    ppermute x6, starting transfers between devices, over_dp(): return lax.ppermute(array, 'dp', [(i, target(i)) for i in range(count)])  7.94 us
    ppermute x14, waiting for transfers between devices, swap(): return lax.ppermute(array, 'tensor', [(0, 1), (1, 0)])  5.39 us
  transfers between devices with their start and end apart: 32, of which 13 were waited for; matrix products, arithmetic and copies ran while one was open for 4% of the time, Pallas kernels for 33%

profile of v2, /device:TPU:0, one launch (start us, length us, event | category | flops | bytes accessed | tf_op | source)
XLA Modules:
  0.0 181.0 jit_solution(675973425286967082)
XLA Ops:
  3.1 3.1 %collective-permute-start = (bf16[48,1280]{1,0:T(8,128)(2,1)S(1)}, bf16[48,1280]{1,0:T(8,128)(2,1)S(1)}, u32[]{:S(2)}, u32[]{:S(2)}) collective-permute-start(bf16[48,1280]{1,0:T(8,128)(2,1)S(1)} %concatenate.46), channel_id=1, source_target_pairs={{0,8},{1,17},{2,10},{3,19},{4,12},{5,21},{6,14},{7,23},{8,0},{9,25... | collective-permute-start | bytes 368648 | tf_op jit(solution)/shard_map/ppermute | solution.py:560
  6.2 1.2 constant_dynamic-slice_fusion.1
  8.3 1.6 collective-permute-start.2
  10.9 2.1 %collective-permute-done.2 = bf16[48,1024]{1,0:T(8,128)(2,1)S(1)} collective-permute-done((bf16[48,1024]{1,0:T(8,128)(2,1)S(1)}, bf16[48,1024]{1,0:T(8,128)(2,1)S(1)}, u32[]{:S(2)}, u32[]{:S(2)}) %collective-permute-start.2) | collective-permute-done | bytes 98336 | tf_op jit(solution)/shard_map/ppermute | solution.py:560
  13.0 1.9 %collective-permute-start.1 = (bf16[96,1280]{1,0:T(8,128)(2,1)S(1)}, bf16[96,1280]{1,0:T(8,128)(2,1)S(1)}, u32[]{:S(2)}, u32[]{:S(2)}) collective-permute-start(bf16[96,1280]{1,0:T(8,128)(2,1)S(1)} %pad_maximum_fusion.6), channel_id=1, source_target_pairs={{0,16},{1,9},{2,18},{3,11},{4,20},{5,13},{6,22},{7,15},{8,24},{9,1... | collective-permute-start | bytes 737288 | tf_op jit(solution)/shard_map/ppermute | solution.py:560
  14.9 1.5 collective-permute-start.3
  17.1 3.5 %collective-permute-done.3 = bf16[96,1024]{1,0:T(8,128)(2,1)S(1)} collective-permute-done((bf16[96,1024]{1,0:T(8,128)(2,1)S(1)}, bf16[96,1024]{1,0:T(8,128)(2,1)S(1)}, u32[]{:S(2)}, u32[]{:S(2)}) %collective-permute-start.3) | collective-permute-done | bytes 196640 | tf_op jit(solution)/shard_map/ppermute | solution.py:560
  20.6 2.2 %collective-permute-done.1 = bf16[96,1280]{1,0:T(8,128)(2,1)S(1)} collective-permute-done((bf16[96,1280]{1,0:T(8,128)(2,1)S(1)}, bf16[96,1280]{1,0:T(8,128)(2,1)S(1)}, u32[]{:S(2)}, u32[]{:S(2)}) %collective-permute-start.1) | collective-permute-done | bytes 245792 | tf_op jit(solution)/shard_map/ppermute | solution.py:560
  22.9 1.6 collective-permute-start.10
  24.6 7.2 %collective-permute-done.10 = bf16[192,1280]{1,0:T(8,128)(2,1)S(1)} collective-permute-done((bf16[192,1280]{1,0:T(8,128)(2,1)S(1)}, bf16[192,1280]{1,0:T(8,128)(2,1)S(1)}, u32[]{:S(2)}, u32[]{:S(2)}) %collective-permute-start.10) | collective-permute-done | bytes 491552 | tf_op jit(solution)/shard_map/ppermute | solution.py:560
  31.9 1.6 collective-permute-start.12
  33.6 14.0 %collective-permute-done.11 = bf16[96,2432]{1,0:T(8,128)(2,1)S(1)} collective-permute-done((bf16[96,2432]{1,0:T(8,128)(2,1)S(1)}, bf16[96,2432]{1,0:T(8,128)(2,1)S(1)}, u32[]{:S(2)}, u32[]{:S(2)}) %collective-permute-start.11) | collective-permute-done | bytes 466976 | tf_op jit(solution)/shard_map/ppermute | solution.py:560
  47.8 1.6 collective-permute-start.16
  49.4 11.2 %collective-permute-done.15 = bf16[192,1024]{1,0:T(8,128)(2,1)S(1)} collective-permute-done((bf16[192,1024]{1,0:T(8,128)(2,1)S(1)}, bf16[192,1024]{1,0:T(8,128)(2,1)S(1)}, u32[]{:S(2)}, u32[]{:S(2)}) %collective-permute-start.15) | collective-permute-done | bytes 393248 | tf_op jit(solution)/shard_map/ppermute | solution.py:560
  63.6 21.9 %project_attend.1 = (bf16[2,512,2304]{2,1,0:T(8,128)(2,1)}, bf16[2,512,768]{2,1,0:T(8,128)(2,1)}, bf16[2,512,128]{2,1,0:T(8,128)(2,1)}, bf16[2,512,256]{2,1,0:T(8,128)(2,1)}) custom-call(s32[64]{0:T(128)} %pad_add_fusion.offsets, s32[2]{0:T(128)} %get-tuple-element.109.lengths, s32[2]{0:T(128)} %get-tuple-element.110.bounds, s32[1]{0:T(128)} %bitcast.2.core_ref, ...), custom_call_target="tpu_custom_call" | custom-call | flops 11274289152 | bytes 9437184 | tf_op jit(solution)/shard_map/project_attend/pallas_call | solution.py:457
  86.8 3.9 %collective-permute-done.21.refs_6_ = bf16[384,1024]{1,0:T(8,128)(2,1)S(1)} collective-permute-done((bf16[384,1024]{1,0:T(8,128)(2,1)S(1)}, bf16[384,1024]{1,0:T(8,128)(2,1)S(1)}, u32[]{:S(2)}, u32[]{:S(2)}) %collective-permute-start.21) | collective-permute-done | bytes 786464 | tf_op jit(solution)/shard_map/ppermute | solution.py:474
  92.8 36.4 %feed.1 = (bf16[4,256,768]{2,1,0:T(8,128)(2,1)}, bf16[2,256,768]{2,1,0:T(8,128)(2,1)}, f32[2,512,768]{2,1,0:T(8,128)}, bf16[2,512,768]{2,1,0:T(8,128)(2,1)}) custom-call(s32[64]{0:T(128)} %pad_add_fusion.offsets, s32[1]{0:T(128)} %bitcast.2.core_ref, bf16[384,2432]{1,0:T(8,128)(2,1)} %copy-done, bf16[384,2432]{1,0:T(8,128)(2,1)} %collective-permute-done.17.refs_1_, ...), custom_call_target="tpu_custom_call" | custom-call | flops 21743271936 | bytes 9437184 | tf_op jit(solution)/shard_map/feed/pallas_call | solution.py:457
  129.4 26.1 %attend_back.1 = (bf16[2,512,2304]{2,1,0:T(8,128)(2,1)}, f32[16,768]{1,0:T(8,128)}) custom-call(s32[2]{0:T(128)} %get-tuple-element.109.lengths, s32[2]{0:T(128)} %get-tuple-element.110.bounds, s32[1]{0:T(128)} %bitcast.2.core_ref, bf16[2,512,2304]{2,1,0:T(8,128)(2,1)} %get-tuple-element.67.refs_0_, bf16[2,512,768]{2,1,0:T(8,128)(2,1)} %get-tuple-element.68.refs_10_.refs_1_, ...), custom_call_target="tpu_custom_call" | custom-call | flops 16106127360 | bytes 12582912 | tf_op jit(solution)/shard_map/attend_back/pallas_call | solution.py:457
  155.5 1.9 %collective-permute-start.25 = (f32[16,768]{1,0:T(8,128)}, f32[16,768]{1,0:T(8,128)S(1)}, u32[]{:S(2)}, u32[]{:S(2)}) collective-permute-start(f32[16,768]{1,0:T(8,128)} %get-tuple-element.80), channel_id=1, source_target_pairs={{0,24},{2,26},{4,28},{6,30},{8,16},{10,18},{12,20},{14,22},{16,8},... | collective-permute-start | bytes 147464 | tf_op jit(solution)/shard_map/ppermute | solution.py:482
  157.4 1.5 collective-permute-start.24
  159.9 12.1 %input_grad.1 = (f32[4,256,768]{2,1,0:T(8,128)}, f32[2,256,768]{2,1,0:T(8,128)}) custom-call(s32[64]{0:T(128)} %pad_add_fusion.offsets, s32[1]{0:T(128)} %bitcast.2.core_ref, bf16[384,1280]{1,0:T(8,128)(2,1)} %copy-done.3, bf16[384,1280]{1,0:T(8,128)(2,1)} %collective-permute-done.12.refs_1_, bf16[384,1280]{1,0:T(8,128)(2,1)} %copy-done.14, ...), custom_call_target="tpu_custom_call" | custom-call | flops 3623878656 | bytes 9437184 | tf_op jit(solution)/shard_map/input_grad/pallas_call | solution.py:457
  172.1 2.1 %collective-permute-start.29 = (f32[16,768]{1,0:T(8,128)S(1)}, f32[16,768]{1,0:T(8,128)S(1)}, u32[]{:S(2)}, u32[]{:S(2)}) collective-permute-start(f32[16,768]{1,0:T(8,128)S(1)} %add_add_fusion.1), channel_id=1, source_target_pairs={{0,6},{2,4},{4,2},{6,0},{8,14},{10,12},{12,10},{14,8},{16,22},{18,... | collective-permute-start | bytes 147464 | tf_op jit(solution)/shard_map/ppermute | solution.py:482
  175.8 1.3 constant_dynamic-update-slice_fusion.9
  179.2 1.2 collective-permute-done.31
  (135 shorter events, 17.2 us)
Async XLA Ops:
  0.7 10.0 %collective-permute-start.8 = (f32[2,384]{1,0:T(2,128)}, f32[2,384]{1,0:T(2,128)S(1)}, u32[]{:S(2)}, u32[]{:S(2)}) collective-permute-start(f32[2,384]{1,0:T(2,128)} %param.23), channel_id=1, source_target_pairs={{0,1},{1,0},{2,3},{3,2},{4,5},{5,4},{6,7},{7,6},{8,9},{9,8},{10,11... | collective-permute-start | bytes 9224 | tf_op jit(solution)/shard_map/ppermute | solution.py:474
  1.2 21.6 %collective-permute-start.7 = (f32[1536]{0:T(1024)}, f32[1536]{0:T(1024)S(1)}, u32[]{:S(2)}, u32[]{:S(2)}) collective-permute-start(f32[1536]{0:T(1024)} %param.28), channel_id=1, source_target_pairs={{0,1},{1,0},{2,3},{3,2},{4,5},{5,4},{6,7},{7,6},{8,9},{9,8},{10,11... | collective-permute-start | bytes 18440 | tf_op jit(solution)/shard_map/ppermute | solution.py:474
  3.1 9.9 %collective-permute-start = (bf16[48,1280]{1,0:T(8,128)(2,1)S(1)}, bf16[48,1280]{1,0:T(8,128)(2,1)S(1)}, u32[]{:S(2)}, u32[]{:S(2)}) collective-permute-start(bf16[48,1280]{1,0:T(8,128)(2,1)S(1)} %concatenate.46), channel_id=1, source_target_pairs={{0,8},{1,17},{2,10},{3,19},{4,12},{5,21},{6,14},{7,23},{8,0},{9,25... | collective-permute-start | bytes 368648 | tf_op jit(solution)/shard_map/ppermute | solution.py:560
  7.4 15.5 %collective-permute-start.4 = (bf16[2,256,768]{2,1,0:T(8,128)(2,1)S(1)}, bf16[2,256,768]{2,1,0:T(8,128)(2,1)}, u32[]{:S(2)}, u32[]{:S(2)}) collective-permute-start(bf16[2,256,768]{2,1,0:T(8,128)(2,1)S(1)} %constant_dynamic-slice_fusion.1), channel_id=1, source_target_pairs={{0,1},{1,0},{2,3},{3,2},{4,5},{5,4},{6,7},{7,6},{8,9},{9,8},{10,11... | collective-permute-start | bytes 2359304 | tf_op jit(solution)/shard_map/ppermute | solution.py:474
  10.7 12.2 %collective-permute-start.6 = (bf16[2,256,768]{2,1,0:T(8,128)(2,1)S(1)}, bf16[2,256,768]{2,1,0:T(8,128)(2,1)S(1)}, u32[]{:S(2)}, u32[]{:S(2)}) collective-permute-start(bf16[2,256,768]{2,1,0:T(8,128)(2,1)S(1)} %constant_dynamic-slice_fusion), channel_id=1, source_target_pairs={{0,1},{1,0},{2,3},{3,2},{4,5},{5,4},{6,7},{7,6},{8,9},{9,8},{10,11... | collective-permute-start | bytes 2359304 | tf_op jit(solution)/shard_map/ppermute | solution.py:474
  13.0 9.8 %collective-permute-start.1 = (bf16[96,1280]{1,0:T(8,128)(2,1)S(1)}, bf16[96,1280]{1,0:T(8,128)(2,1)S(1)}, u32[]{:S(2)}, u32[]{:S(2)}) collective-permute-start(bf16[96,1280]{1,0:T(8,128)(2,1)S(1)} %pad_maximum_fusion.6), channel_id=1, source_target_pairs={{0,16},{1,9},{2,18},{3,11},{4,20},{5,13},{6,22},{7,15},{8,24},{9,1... | collective-permute-start | bytes 737288 | tf_op jit(solution)/shard_map/ppermute | solution.py:560
  14.9 5.7 %collective-permute-start.3 = (bf16[96,1024]{1,0:T(8,128)(2,1)S(1)}, bf16[96,1024]{1,0:T(8,128)(2,1)S(1)}, u32[]{:S(2)}, u32[]{:S(2)}) collective-permute-start(bf16[96,1024]{1,0:T(8,128)(2,1)S(1)} %pad_maximum_fusion.8), channel_id=1, source_target_pairs={{0,4},{1,3},{2,6},{3,1},{4,0},{5,7},{6,2},{7,5},{8,12},{9,11},{10,... | collective-permute-start | bytes 589832 | tf_op jit(solution)/shard_map/ppermute | solution.py:560
  22.9 8.9 %collective-permute-start.10 = (bf16[192,1280]{1,0:T(8,128)(2,1)S(1)}, bf16[192,1280]{1,0:T(8,128)(2,1)S(1)}, u32[]{:S(2)}, u32[]{:S(2)}) collective-permute-start(bf16[192,1280]{1,0:T(8,128)(2,1)S(1)} %pad_maximum_fusion.3), channel_id=1, source_target_pairs={{0,2},{1,5},{2,0},{3,7},{4,6},{5,1},{6,4},{7,3},{8,10},{9,13},{10,... | collective-permute-start | bytes 1474568 | tf_op jit(solution)/shard_map/ppermute | solution.py:560
  24.5 9.0 %collective-permute-start.9 = (bf16[48,2432]{1,0:T(8,128)(2,1)S(1)}, bf16[48,2432]{1,0:T(8,128)(2,1)S(1)}, u32[]{:S(2)}, u32[]{:S(2)}) collective-permute-start(bf16[48,2432]{1,0:T(8,128)(2,1)S(1)} %pad_maximum_fusion.7), channel_id=1, source_target_pairs={{0,8},{1,17},{2,10},{3,19},{4,12},{5,21},{6,14},{7,23},{8,0},{9,25... | collective-permute-start | bytes 700424 | tf_op jit(solution)/shard_map/ppermute | solution.py:560
  31.9 15.9 %collective-permute-start.13 = (bf16[384,1280]{1,0:T(8,128)(2,1)S(1)}, bf16[384,1280]{1,0:T(8,128)(2,1)S(1)}, u32[]{:S(2)}, u32[]{:S(2)}) collective-permute-start(bf16[384,1280]{1,0:T(8,128)(2,1)S(1)} %constant_dynamic-update-slice_fusion.1.refs_0_), channel_id=1, source_target_pairs={{0,1},{1,0},{2,3},{3,2},{4,5},{5,4},{6,7},{7,6},{8,9},{9,8},{10,11... | collective-permute-start | bytes 2949128 | tf_op jit(solution)/shard_map/ppermute | solution.py:474
  31.9 15.9 %collective-permute-start.12 = (bf16[384,1280]{1,0:T(8,128)(2,1)S(1)}, bf16[384,1280]{1,0:T(8,128)(2,1)}, u32[]{:S(2)}, u32[]{:S(2)}) collective-permute-start(bf16[384,1280]{1,0:T(8,128)(2,1)S(1)} %constant_dynamic-update-slice_fusion.1.refs_0_), channel_id=1, source_target_pairs={{0,4},{1,3},{2,6},{3,1},{4,0},{5,7},{6,2},{7,5},{8,12},{9,11},{10,... | collective-permute-start | bytes 2949128 | tf_op jit(solution)/shard_map/ppermute | solution.py:560
  33.6 14.1 %collective-permute-start.11 = (bf16[96,2432]{1,0:T(8,128)(2,1)S(1)}, bf16[96,2432]{1,0:T(8,128)(2,1)S(1)}, u32[]{:S(2)}, u32[]{:S(2)}) collective-permute-start(bf16[96,2432]{1,0:T(8,128)(2,1)S(1)} %pad_maximum_fusion.4), channel_id=1, source_target_pairs={{0,16},{1,9},{2,18},{3,11},{4,20},{5,13},{6,22},{7,15},{8,24},{9,1... | collective-permute-start | bytes 1400840 | tf_op jit(solution)/shard_map/ppermute | solution.py:560
  47.8 13.6 %collective-permute-start.16 = (bf16[192,2432]{1,0:T(8,128)(2,1)S(1)}, bf16[192,2432]{1,0:T(8,128)(2,1)S(1)}, u32[]{:S(2)}, u32[]{:S(2)}) collective-permute-start(bf16[192,2432]{1,0:T(8,128)(2,1)S(1)} %pad_maximum_fusion.1), channel_id=1, source_target_pairs={{0,2},{1,5},{2,0},{3,7},{4,6},{5,1},{6,4},{7,3},{8,10},{9,13},{10,... | collective-permute-start | bytes 2801672 | tf_op jit(solution)/shard_map/ppermute | solution.py:560
  49.3 11.2 %collective-permute-start.15 = (bf16[192,1024]{1,0:T(8,128)(2,1)S(1)}, bf16[192,1024]{1,0:T(8,128)(2,1)S(1)}, u32[]{:S(2)}, u32[]{:S(2)}) collective-permute-start(bf16[192,1024]{1,0:T(8,128)(2,1)S(1)} %pad_maximum_fusion.5), channel_id=1, source_target_pairs={{0,8},{1,17},{2,10},{3,19},{4,12},{5,21},{6,14},{7,23},{8,0},{9,25... | collective-permute-start | bytes 1179656 | tf_op jit(solution)/shard_map/ppermute | solution.py:560
  49.3 14.3 %collective-permute-start.14 = (bf16[384,1280]{1,0:T(8,128)(2,1)}, bf16[384,1280]{1,0:T(8,128)(2,1)}, u32[]{:S(2)}, u32[]{:S(2)}) collective-permute-start(bf16[384,1280]{1,0:T(8,128)(2,1)} %collective-permute-done.12.refs_1_), channel_id=1, source_target_pairs={{0,1},{1,0},{2,3},{3,2},{4,5},{5,4},{6,7},{7,6},{8,9},{9,8},{10,11... | collective-permute-start | bytes 2949128 | tf_op jit(solution)/shard_map/ppermute | solution.py:474
  61.6 23.9 %collective-permute-start.17 = (bf16[384,2432]{1,0:T(8,128)(2,1)S(1)}, bf16[384,2432]{1,0:T(8,128)(2,1)}, u32[]{:S(2)}, u32[]{:S(2)}) collective-permute-start(bf16[384,2432]{1,0:T(8,128)(2,1)S(1)} %pad_maximum_fusion.refs_0_), channel_id=1, source_target_pairs={{0,4},{1,3},{2,6},{3,1},{4,0},{5,7},{6,2},{7,5},{8,12},{9,11},{10,... | collective-permute-start | bytes 5603336 | tf_op jit(solution)/shard_map/ppermute | solution.py:560
  63.1 27.6 %collective-permute-start.19 = (bf16[384,2432]{1,0:T(8,128)(2,1)S(1)}, bf16[384,2432]{1,0:T(8,128)(2,1)}, u32[]{:S(2)}, u32[]{:S(2)}) collective-permute-start(bf16[384,2432]{1,0:T(8,128)(2,1)S(1)} %pad_maximum_fusion.refs_0_), channel_id=1, source_target_pairs={{0,1},{1,0},{2,3},{3,2},{4,5},{5,4},{6,7},{7,6},{8,9},{9,8},{10,11... | collective-permute-start | bytes 5603336 | tf_op jit(solution)/shard_map/ppermute | solution.py:474
  63.1 22.4 %collective-permute-start.18 = (bf16[384,1024]{1,0:T(8,128)(2,1)S(1)}, bf16[384,1024]{1,0:T(8,128)(2,1)}, u32[]{:S(2)}, u32[]{:S(2)}) collective-permute-start(bf16[384,1024]{1,0:T(8,128)(2,1)S(1)} %pad_maximum_fusion.2.refs_4_), channel_id=1, source_target_pairs={{0,16},{1,9},{2,18},{3,11},{4,20},{5,13},{6,22},{7,15},{8,24},{9,1... | collective-permute-start | bytes 2359304 | tf_op jit(solution)/shard_map/ppermute | solution.py:560
  85.5 7.3 %collective-permute-start.20 = (bf16[384,2432]{1,0:T(8,128)(2,1)}, bf16[384,2432]{1,0:T(8,128)(2,1)}, u32[]{:S(2)}, u32[]{:S(2)}) collective-permute-start(bf16[384,2432]{1,0:T(8,128)(2,1)} %collective-permute-done.17.refs_1_), channel_id=1, source_target_pairs={{0,1},{1,0},{2,3},{3,2},{4,5},{5,4},{6,7},{7,6},{8,9},{9,8},{10,11... | collective-permute-start | bytes 5603336 | tf_op jit(solution)/shard_map/ppermute | solution.py:474
  86.1 5.8 %collective-permute-start.22 = (bf16[384,1024]{1,0:T(8,128)(2,1)}, bf16[384,1024]{1,0:T(8,128)(2,1)S(1)}, u32[]{:S(2)}, u32[]{:S(2)}) collective-permute-start(bf16[384,1024]{1,0:T(8,128)(2,1)} %collective-permute-done.18.refs_5_), channel_id=1, source_target_pairs={{0,1},{1,0},{2,3},{3,2},{4,5},{5,4},{6,7},{7,6},{8,9},{9,8},{10,11... | collective-permute-start | bytes 2359304 | tf_op jit(solution)/shard_map/ppermute | solution.py:474
  129.2 30.7 %collective-permute-start.26 = (bf16[2,256,768]{2,1,0:T(8,128)(2,1)}, bf16[2,256,768]{2,1,0:T(8,128)(2,1)S(1)}, u32[]{:S(2)}, u32[]{:S(2)}) collective-permute-start(bf16[2,256,768]{2,1,0:T(8,128)(2,1)} %get-tuple-element.82), channel_id=1, source_target_pairs={{0,1},{1,0},{2,3},{3,2},{4,5},{5,4},{6,7},{7,6},{8,9},{9,8},{10,11... | collective-permute-start | bytes 2359304 | tf_op jit(solution)/shard_map/ppermute | solution.py:474
  155.5 16.5 %collective-permute-start.25 = (f32[16,768]{1,0:T(8,128)}, f32[16,768]{1,0:T(8,128)S(1)}, u32[]{:S(2)}, u32[]{:S(2)}) collective-permute-start(f32[16,768]{1,0:T(8,128)} %get-tuple-element.80), channel_id=1, source_target_pairs={{0,24},{2,26},{4,28},{6,30},{8,16},{10,18},{12,20},{14,22},{16,8},... | collective-permute-start | bytes 147464 | tf_op jit(solution)/shard_map/ppermute | solution.py:482
  157.4 14.6 %collective-permute-start.24 = (f32[16,768]{1,0:T(8,128)}, f32[16,768]{1,0:T(8,128)S(1)}, u32[]{:S(2)}, u32[]{:S(2)}) collective-permute-start(f32[16,768]{1,0:T(8,128)} %get-tuple-element.80), channel_id=1, source_target_pairs={{0,16},{2,18},{4,20},{6,22},{8,24},{10,26},{12,28},{14,30},{16,0},... | collective-permute-start | bytes 147464 | tf_op jit(solution)/shard_map/ppermute | solution.py:482
  158.9 13.1 %collective-permute-start.23 = (f32[16,768]{1,0:T(8,128)}, f32[16,768]{1,0:T(8,128)S(1)}, u32[]{:S(2)}, u32[]{:S(2)}) collective-permute-start(f32[16,768]{1,0:T(8,128)} %get-tuple-element.80), channel_id=1, source_target_pairs={{0,8},{2,10},{4,12},{6,14},{8,0},{10,2},{12,4},{14,6},{16,24},{18,... | collective-permute-start | bytes 147464 | tf_op jit(solution)/shard_map/ppermute | solution.py:482
  (30 other events, 316.9 us)

commit v3 on v2

--- a/solution.py
+++ b/solution.py
@@ -538,6 +538,9 @@
     grad_got = swap(lax.dynamic_slice_in_dim(output_gradient, others, mine, 0))
     bias_got, up_got, hidden_bias_got = map(swap, (query_value_bias, adapter_up_weight, feedforward_input_bias))
 
+    first_item = core * mine
+    my_lengths = lax.dynamic_slice_in_dim(lengths[:, 0], first_item, mine, 0)
+    my_bounds = lax.dynamic_slice_in_dim(bounds[:, 0], first_item, mine, 0)
     blank = jnp.zeros((heads,), F32)
     ones = blank + 1
     both = [query_value_bias[0], blank, query_value_bias[1], bias_got[0], blank, bias_got[1]]
@@ -577,14 +580,18 @@
         line_first = joined(line_first, exchange(line_first, LINE_FIRST, 1))
         own = [line, exchange(line, LINE_FIRST, 3)]
         swapped = [swap(line)]
-        line_first, plane, own, swapped = lax.optimization_barrier((line_first, plane, own, swapped))
+        line_first, plane, own, swapped, my_lengths, my_bounds = lax.optimization_barrier(
+            (line_first, plane, own, swapped, my_lengths, my_bounds)
+        )
         swapped.append(swap(own[1]))
         line_first = joined(line_first, exchange(line_first, LINE_FIRST, 2))
         plane = joined(plane, exchange(plane, PLANE_FIRST, 2))
+        got_last = [swap(plane)]
         plane, line_first, x_got = lax.optimization_barrier((plane, line_first, x_got))
         own_first = [line_first, exchange(line_first, LINE_FIRST, 3)]
         own_last = [plane, exchange(plane, PLANE_FIRST, 3)]
-        got_first, got_last = [swap(line_first)], [swap(plane)]
+        got_first = [swap(line_first)]
+        got_last, x_got = lax.optimization_barrier((got_last, x_got))
     else:
         offsets = jnp.zeros((2,), jnp.int32)
         order = order_last = ((0, 0), 1)
@@ -595,9 +602,6 @@
         swapped, got_first, got_last = [swap(own[0])], [], []
     pieces = (*own, *swapped)
 
-    first_item = core * mine
-    my_lengths = lax.dynamic_slice_in_dim(lengths[:, 0], first_item, mine, 0)
-    my_bounds = lax.dynamic_slice_in_dim(bounds[:, 0], first_item, mine, 0)
     core = core[None].astype(jnp.int32)
 
     own_block = pl.BlockSpec((1, rows, width), lambda i, *s: (s[-1][0] * mine + i, 0, 0))

time: 181 us -> 184 us (1.017)
  local copies, waits for them, and re-layouts: 7.1 us -> 9.5 us
    unnamed x48 -> x51, local copies, waits for them, and re-layouts: 2.14 us -> 4.45 us
where the time goes in v3:
time: 184 us
  Pallas kernels  96.4 us (52%)
  waiting for transfers between devices  48.6 us (26%)
  starting transfers between devices  25.4 us (14%)
  local copies, waits for them, and re-layouts  9.5 us (5%)
  other arithmetic  2.91 us (2%)
    pallas_call x4, Pallas kernels, call(): pl.pallas_call(kernel, grid_spec=pltpu.PrefetchScalarGridSpec(num_scalar_...  96.4 us
    ppermute x12, waiting for transfers between devices, exchange(): return lax.ppermute(array, ('dp', 'tensor'), pairs)  40.3 us
    ppermute x12, starting transfers between devices, exchange(): return lax.ppermute(array, ('dp', 'tensor'), pairs)  14.4 us
    ppermute x6, starting transfers between devices, over_dp(): return lax.ppermute(array, 'dp', [(i, target(i)) for i in range(count)])  7.94 us
    ppermute x14, waiting for transfers between devices, swap(): return lax.ppermute(array, 'tensor', [(0, 1), (1, 0)])  6.5 us
    unnamed x51, local copies, waits for them, and re-layouts  4.45 us
  transfers between devices with their start and end apart: 32, of which 13 were waited for; matrix products, arithmetic and copies ran while one was open for 4% of the time, Pallas kernels for 33%

profile of v3, /device:TPU:0, one launch (start us, length us, event | category | flops | bytes accessed | tf_op | source)
XLA Modules:
  0.0 184.0 jit_solution(1879615804232668040)
XLA Ops:
  3.1 3.1 %collective-permute-start = (bf16[48,1280]{1,0:T(8,128)(2,1)S(1)}, bf16[48,1280]{1,0:T(8,128)(2,1)S(1)}, u32[]{:S(2)}, u32[]{:S(2)}) collective-permute-start(bf16[48,1280]{1,0:T(8,128)(2,1)S(1)} %concatenate.47), channel_id=1, source_target_pairs={{0,8},{1,17},{2,10},{3,19},{4,12},{5,21},{6,14},{7,23},{8,0},{9,25... | collective-permute-start | bytes 368648 | tf_op jit(solution)/shard_map/ppermute | solution.py:563
  8.3 1.6 collective-permute-start.2
  10.9 2.1 %collective-permute-done.2 = bf16[48,1024]{1,0:T(8,128)(2,1)S(1)} collective-permute-done((bf16[48,1024]{1,0:T(8,128)(2,1)S(1)}, bf16[48,1024]{1,0:T(8,128)(2,1)S(1)}, u32[]{:S(2)}, u32[]{:S(2)}) %collective-permute-start.2) | collective-permute-done | bytes 98336 | tf_op jit(solution)/shard_map/ppermute | solution.py:563
  13.0 1.9 %collective-permute-start.1 = (bf16[96,1280]{1,0:T(8,128)(2,1)S(1)}, bf16[96,1280]{1,0:T(8,128)(2,1)S(1)}, u32[]{:S(2)}, u32[]{:S(2)}) collective-permute-start(bf16[96,1280]{1,0:T(8,128)(2,1)S(1)} %pad_maximum_fusion.5), channel_id=1, source_target_pairs={{0,16},{1,9},{2,18},{3,11},{4,20},{5,13},{6,22},{7,15},{8,24},{9,1... | collective-permute-start | bytes 737288 | tf_op jit(solution)/shard_map/ppermute | solution.py:563
  14.9 1.5 collective-permute-start.3
  17.1 3.5 %collective-permute-done.3 = bf16[96,1024]{1,0:T(8,128)(2,1)S(1)} collective-permute-done((bf16[96,1024]{1,0:T(8,128)(2,1)S(1)}, bf16[96,1024]{1,0:T(8,128)(2,1)S(1)}, u32[]{:S(2)}, u32[]{:S(2)}) %collective-permute-start.3) | collective-permute-done | bytes 196640 | tf_op jit(solution)/shard_map/ppermute | solution.py:563
  20.6 2.2 %collective-permute-done.1 = bf16[96,1280]{1,0:T(8,128)(2,1)S(1)} collective-permute-done((bf16[96,1280]{1,0:T(8,128)(2,1)S(1)}, bf16[96,1280]{1,0:T(8,128)(2,1)S(1)}, u32[]{:S(2)}, u32[]{:S(2)}) %collective-permute-start.1) | collective-permute-done | bytes 245792 | tf_op jit(solution)/shard_map/ppermute | solution.py:563
  22.9 1.6 collective-permute-start.10
  24.6 7.2 %collective-permute-done.10 = bf16[192,1280]{1,0:T(8,128)(2,1)S(1)} collective-permute-done((bf16[192,1280]{1,0:T(8,128)(2,1)S(1)}, bf16[192,1280]{1,0:T(8,128)(2,1)S(1)}, u32[]{:S(2)}, u32[]{:S(2)}) %collective-permute-start.10) | collective-permute-done | bytes 491552 | tf_op jit(solution)/shard_map/ppermute | solution.py:563
  32.0 1.6 collective-permute-start.12
  34.3 13.3 %collective-permute-done.11 = bf16[96,2432]{1,0:T(8,128)(2,1)S(1)} collective-permute-done((bf16[96,2432]{1,0:T(8,128)(2,1)S(1)}, bf16[96,2432]{1,0:T(8,128)(2,1)S(1)}, u32[]{:S(2)}, u32[]{:S(2)}) %collective-permute-start.11) | collective-permute-done | bytes 466976 | tf_op jit(solution)/shard_map/ppermute | solution.py:563
  47.8 1.6 collective-permute-start.17
  49.4 11.2 %collective-permute-done.15 = bf16[192,1024]{1,0:T(8,128)(2,1)S(1)} collective-permute-done((bf16[192,1024]{1,0:T(8,128)(2,1)S(1)}, bf16[192,1024]{1,0:T(8,128)(2,1)S(1)}, u32[]{:S(2)}, u32[]{:S(2)}) %collective-permute-start.15) | collective-permute-done | bytes 393248 | tf_op jit(solution)/shard_map/ppermute | solution.py:563
  63.6 1.3 collective-permute-done.16.refs_6_
  66.7 21.9 %project_attend.1 = (bf16[2,512,2304]{2,1,0:T(8,128)(2,1)}, bf16[2,512,768]{2,1,0:T(8,128)(2,1)}, bf16[2,512,128]{2,1,0:T(8,128)(2,1)}, bf16[2,512,256]{2,1,0:T(8,128)(2,1)}) custom-call(s32[64]{0:T(128)} %pad_add_fusion.offsets, s32[2]{0:T(128)} %get-tuple-element.61.lengths, s32[2]{0:T(128)} %get-tuple-element.62.bounds, s32[1]{0:T(128)} %bitcast.6.core_ref, ...), custom_call_target="tpu_custom_call" | custom-call | flops 11274289152 | bytes 9437184 | tf_op jit(solution)/shard_map/project_attend/pallas_call | solution.py:457
  89.8 4.0 %collective-permute-done.22.refs_7_ = bf16[384,1024]{1,0:T(8,128)(2,1)S(1)} collective-permute-done((bf16[384,1024]{1,0:T(8,128)(2,1)}, bf16[384,1024]{1,0:T(8,128)(2,1)S(1)}, u32[]{:S(2)}, u32[]{:S(2)}) %collective-permute-start.22) | collective-permute-done | bytes 786464 | tf_op jit(solution)/shard_map/ppermute | solution.py:474
  94.7 1.3 copy-done.12
  96.0 36.4 %feed.1 = (bf16[4,256,768]{2,1,0:T(8,128)(2,1)}, bf16[2,256,768]{2,1,0:T(8,128)(2,1)}, f32[2,512,768]{2,1,0:T(8,128)}, bf16[2,512,768]{2,1,0:T(8,128)(2,1)}) custom-call(s32[64]{0:T(128)} %pad_add_fusion.offsets, s32[1]{0:T(128)} %bitcast.6.core_ref, bf16[384,2432]{1,0:T(8,128)(2,1)} %copy-done, bf16[384,2432]{1,0:T(8,128)(2,1)} %collective-permute-done.18.refs_1_, ...), custom_call_target="tpu_custom_call" | custom-call | flops 21743271936 | bytes 9437184 | tf_op jit(solution)/shard_map/feed/pallas_call | solution.py:457
  132.7 26.1 %attend_back.1 = (bf16[2,512,2304]{2,1,0:T(8,128)(2,1)}, f32[16,768]{1,0:T(8,128)}) custom-call(s32[2]{0:T(128)} %get-tuple-element.61.lengths, s32[2]{0:T(128)} %get-tuple-element.62.bounds, s32[1]{0:T(128)} %bitcast.6.core_ref, bf16[2,512,2304]{2,1,0:T(8,128)(2,1)} %get-tuple-element.74.refs_0_, bf16[2,512,768]{2,1,0:T(8,128)(2,1)} %get-tuple-element.75.refs_10_.refs_1_, ...), custom_call_target="tpu_custom_call" | custom-call | flops 16106127360 | bytes 12582912 | tf_op jit(solution)/shard_map/attend_back/pallas_call | solution.py:457
  158.8 1.9 %collective-permute-start.25 = (f32[16,768]{1,0:T(8,128)}, f32[16,768]{1,0:T(8,128)S(1)}, u32[]{:S(2)}, u32[]{:S(2)}) collective-permute-start(f32[16,768]{1,0:T(8,128)} %get-tuple-element.88), channel_id=1, source_target_pairs={{0,24},{2,26},{4,28},{6,30},{8,16},{10,18},{12,20},{14,22},{16,8},... | collective-permute-start | bytes 147464 | tf_op jit(solution)/shard_map/ppermute | solution.py:482
  160.9 2.3 %collective-permute-start.23 = (f32[16,768]{1,0:T(8,128)}, f32[16,768]{1,0:T(8,128)S(1)}, u32[]{:S(2)}, u32[]{:S(2)}) collective-permute-start(f32[16,768]{1,0:T(8,128)} %get-tuple-element.88), channel_id=1, source_target_pairs={{0,8},{2,10},{4,12},{6,14},{8,0},{10,2},{12,4},{14,6},{16,24},{18,... | collective-permute-start | bytes 147464 | tf_op jit(solution)/shard_map/ppermute | solution.py:482
  163.2 12.1 %input_grad.1 = (f32[4,256,768]{2,1,0:T(8,128)}, f32[2,256,768]{2,1,0:T(8,128)}) custom-call(s32[64]{0:T(128)} %pad_add_fusion.offsets, s32[1]{0:T(128)} %bitcast.6.core_ref, bf16[384,1280]{1,0:T(8,128)(2,1)} %copy-done.2, bf16[384,1280]{1,0:T(8,128)(2,1)} %collective-permute-done.12.refs_1_, bf16[384,1280]{1,0:T(8,128)(2,1)} %collective-permute-done.13.refs_2_, ...), custom_call_target="tpu_custom_call" | custom-call | flops 3623878656 | bytes 9437184 | tf_op jit(solution)/shard_map/input_grad/pallas_call | solution.py:457
  175.4 2.3 %collective-permute-start.29 = (f32[16,768]{1,0:T(8,128)S(1)}, f32[16,768]{1,0:T(8,128)S(1)}, u32[]{:S(2)}, u32[]{:S(2)}) collective-permute-start(f32[16,768]{1,0:T(8,128)S(1)} %add_add_fusion.1), channel_id=1, source_target_pairs={{0,6},{2,4},{4,2},{6,0},{8,14},{10,12},{12,10},{14,8},{16,22},{18,... | collective-permute-start | bytes 147464 | tf_op jit(solution)/shard_map/ppermute | solution.py:482
  179.0 1.3 constant_dynamic-update-slice_fusion.11
  (138 shorter events, 19.7 us)
Async XLA Ops:
  0.7 10.0 %collective-permute-start.8 = (f32[2,384]{1,0:T(2,128)}, f32[2,384]{1,0:T(2,128)S(1)}, u32[]{:S(2)}, u32[]{:S(2)}) collective-permute-start(f32[2,384]{1,0:T(2,128)} %param.23), channel_id=1, source_target_pairs={{0,1},{1,0},{2,3},{3,2},{4,5},{5,4},{6,7},{7,6},{8,9},{9,8},{10,11... | collective-permute-start | bytes 9224 | tf_op jit(solution)/shard_map/ppermute | solution.py:474
  1.2 21.6 %collective-permute-start.7 = (f32[1536]{0:T(1024)}, f32[1536]{0:T(1024)S(1)}, u32[]{:S(2)}, u32[]{:S(2)}) collective-permute-start(f32[1536]{0:T(1024)} %param.28), channel_id=1, source_target_pairs={{0,1},{1,0},{2,3},{3,2},{4,5},{5,4},{6,7},{7,6},{8,9},{9,8},{10,11... | collective-permute-start | bytes 18440 | tf_op jit(solution)/shard_map/ppermute | solution.py:474
  3.1 9.9 %collective-permute-start = (bf16[48,1280]{1,0:T(8,128)(2,1)S(1)}, bf16[48,1280]{1,0:T(8,128)(2,1)S(1)}, u32[]{:S(2)}, u32[]{:S(2)}) collective-permute-start(bf16[48,1280]{1,0:T(8,128)(2,1)S(1)} %concatenate.47), channel_id=1, source_target_pairs={{0,8},{1,17},{2,10},{3,19},{4,12},{5,21},{6,14},{7,23},{8,0},{9,25... | collective-permute-start | bytes 368648 | tf_op jit(solution)/shard_map/ppermute | solution.py:563
  7.4 15.5 %collective-permute-start.4 = (bf16[2,256,768]{2,1,0:T(8,128)(2,1)S(1)}, bf16[2,256,768]{2,1,0:T(8,128)(2,1)}, u32[]{:S(2)}, u32[]{:S(2)}) collective-permute-start(bf16[2,256,768]{2,1,0:T(8,128)(2,1)S(1)} %constant_dynamic-slice_fusion.3), channel_id=1, source_target_pairs={{0,1},{1,0},{2,3},{3,2},{4,5},{5,4},{6,7},{7,6},{8,9},{9,8},{10,11... | collective-permute-start | bytes 2359304 | tf_op jit(solution)/shard_map/ppermute | solution.py:474
  10.7 12.2 %collective-permute-start.6 = (bf16[2,256,768]{2,1,0:T(8,128)(2,1)S(1)}, bf16[2,256,768]{2,1,0:T(8,128)(2,1)S(1)}, u32[]{:S(2)}, u32[]{:S(2)}) collective-permute-start(bf16[2,256,768]{2,1,0:T(8,128)(2,1)S(1)} %constant_dynamic-slice_fusion.2), channel_id=1, source_target_pairs={{0,1},{1,0},{2,3},{3,2},{4,5},{5,4},{6,7},{7,6},{8,9},{9,8},{10,11... | collective-permute-start | bytes 2359304 | tf_op jit(solution)/shard_map/ppermute | solution.py:474
  13.0 9.8 %collective-permute-start.1 = (bf16[96,1280]{1,0:T(8,128)(2,1)S(1)}, bf16[96,1280]{1,0:T(8,128)(2,1)S(1)}, u32[]{:S(2)}, u32[]{:S(2)}) collective-permute-start(bf16[96,1280]{1,0:T(8,128)(2,1)S(1)} %pad_maximum_fusion.5), channel_id=1, source_target_pairs={{0,16},{1,9},{2,18},{3,11},{4,20},{5,13},{6,22},{7,15},{8,24},{9,1... | collective-permute-start | bytes 737288 | tf_op jit(solution)/shard_map/ppermute | solution.py:563
  14.9 5.7 %collective-permute-start.3 = (bf16[96,1024]{1,0:T(8,128)(2,1)S(1)}, bf16[96,1024]{1,0:T(8,128)(2,1)S(1)}, u32[]{:S(2)}, u32[]{:S(2)}) collective-permute-start(bf16[96,1024]{1,0:T(8,128)(2,1)S(1)} %pad_maximum_fusion.7), channel_id=1, source_target_pairs={{0,4},{1,3},{2,6},{3,1},{4,0},{5,7},{6,2},{7,5},{8,12},{9,11},{10,... | collective-permute-start | bytes 589832 | tf_op jit(solution)/shard_map/ppermute | solution.py:563
  22.9 8.9 %collective-permute-start.10 = (bf16[192,1280]{1,0:T(8,128)(2,1)S(1)}, bf16[192,1280]{1,0:T(8,128)(2,1)S(1)}, u32[]{:S(2)}, u32[]{:S(2)}) collective-permute-start(bf16[192,1280]{1,0:T(8,128)(2,1)S(1)} %pad_maximum_fusion.2), channel_id=1, source_target_pairs={{0,2},{1,5},{2,0},{3,7},{4,6},{5,1},{6,4},{7,3},{8,10},{9,13},{10,... | collective-permute-start | bytes 1474568 | tf_op jit(solution)/shard_map/ppermute | solution.py:563
  24.5 9.0 %collective-permute-start.9 = (bf16[48,2432]{1,0:T(8,128)(2,1)S(1)}, bf16[48,2432]{1,0:T(8,128)(2,1)S(1)}, u32[]{:S(2)}, u32[]{:S(2)}) collective-permute-start(bf16[48,2432]{1,0:T(8,128)(2,1)S(1)} %pad_maximum_fusion.6), channel_id=1, source_target_pairs={{0,8},{1,17},{2,10},{3,19},{4,12},{5,21},{6,14},{7,23},{8,0},{9,25... | collective-permute-start | bytes 700424 | tf_op jit(solution)/shard_map/ppermute | solution.py:563
  31.9 15.9 %collective-permute-start.13 = (bf16[384,1280]{1,0:T(8,128)(2,1)S(1)}, bf16[384,1280]{1,0:T(8,128)(2,1)}, u32[]{:S(2)}, u32[]{:S(2)}) collective-permute-start(bf16[384,1280]{1,0:T(8,128)(2,1)S(1)} %constant_dynamic-update-slice_fusion.1.refs_0_), channel_id=1, source_target_pairs={{0,1},{1,0},{2,3},{3,2},{4,5},{5,4},{6,7},{7,6},{8,9},{9,8},{10,11... | collective-permute-start | bytes 2949128 | tf_op jit(solution)/shard_map/ppermute | solution.py:474
  32.0 15.8 %collective-permute-start.12 = (bf16[384,1280]{1,0:T(8,128)(2,1)S(1)}, bf16[384,1280]{1,0:T(8,128)(2,1)}, u32[]{:S(2)}, u32[]{:S(2)}) collective-permute-start(bf16[384,1280]{1,0:T(8,128)(2,1)S(1)} %constant_dynamic-update-slice_fusion.1.refs_0_), channel_id=1, source_target_pairs={{0,4},{1,3},{2,6},{3,1},{4,0},{5,7},{6,2},{7,5},{8,12},{9,11},{10,... | collective-permute-start | bytes 2949128 | tf_op jit(solution)/shard_map/ppermute | solution.py:563
  33.6 14.1 %collective-permute-start.11 = (bf16[96,2432]{1,0:T(8,128)(2,1)S(1)}, bf16[96,2432]{1,0:T(8,128)(2,1)S(1)}, u32[]{:S(2)}, u32[]{:S(2)}) collective-permute-start(bf16[96,2432]{1,0:T(8,128)(2,1)S(1)} %pad_maximum_fusion.3), channel_id=1, source_target_pairs={{0,16},{1,9},{2,18},{3,11},{4,20},{5,13},{6,22},{7,15},{8,24},{9,1... | collective-permute-start | bytes 1400840 | tf_op jit(solution)/shard_map/ppermute | solution.py:563
  47.8 13.6 %collective-permute-start.17 = (bf16[192,2432]{1,0:T(8,128)(2,1)S(1)}, bf16[192,2432]{1,0:T(8,128)(2,1)S(1)}, u32[]{:S(2)}, u32[]{:S(2)}) collective-permute-start(bf16[192,2432]{1,0:T(8,128)(2,1)S(1)} %pad_maximum_fusion.1), channel_id=1, source_target_pairs={{0,2},{1,5},{2,0},{3,7},{4,6},{5,1},{6,4},{7,3},{8,10},{9,13},{10,... | collective-permute-start | bytes 2801672 | tf_op jit(solution)/shard_map/ppermute | solution.py:563
  49.4 11.2 %collective-permute-start.15 = (bf16[192,1024]{1,0:T(8,128)(2,1)S(1)}, bf16[192,1024]{1,0:T(8,128)(2,1)S(1)}, u32[]{:S(2)}, u32[]{:S(2)}) collective-permute-start(bf16[192,1024]{1,0:T(8,128)(2,1)S(1)} %pad_maximum_fusion.4), channel_id=1, source_target_pairs={{0,8},{1,17},{2,10},{3,19},{4,12},{5,21},{6,14},{7,23},{8,0},{9,25... | collective-permute-start | bytes 1179656 | tf_op jit(solution)/shard_map/ppermute | solution.py:563
  49.4 15.5 %collective-permute-start.14 = (bf16[384,1280]{1,0:T(8,128)(2,1)}, bf16[384,1280]{1,0:T(8,128)(2,1)S(1)}, u32[]{:S(2)}, u32[]{:S(2)}) collective-permute-start(bf16[384,1280]{1,0:T(8,128)(2,1)} %collective-permute-done.12.refs_1_), channel_id=1, source_target_pairs={{0,1},{1,0},{2,3},{3,2},{4,5},{5,4},{6,7},{7,6},{8,9},{9,8},{10,11... | collective-permute-start | bytes 2949128 | tf_op jit(solution)/shard_map/ppermute | solution.py:474
  61.6 27.0 %collective-permute-start.18 = (bf16[384,2432]{1,0:T(8,128)(2,1)S(1)}, bf16[384,2432]{1,0:T(8,128)(2,1)}, u32[]{:S(2)}, u32[]{:S(2)}) collective-permute-start(bf16[384,2432]{1,0:T(8,128)(2,1)S(1)} %pad_maximum_fusion.refs_0_), channel_id=1, source_target_pairs={{0,4},{1,3},{2,6},{3,1},{4,0},{5,7},{6,2},{7,5},{8,12},{9,11},{10,... | collective-permute-start | bytes 5603336 | tf_op jit(solution)/shard_map/ppermute | solution.py:563
  62.5 27.2 %collective-permute-start.20 = (bf16[384,2432]{1,0:T(8,128)(2,1)S(1)}, bf16[384,2432]{1,0:T(8,128)(2,1)}, u32[]{:S(2)}, u32[]{:S(2)}) collective-permute-start(bf16[384,2432]{1,0:T(8,128)(2,1)S(1)} %pad_maximum_fusion.refs_0_), channel_id=1, source_target_pairs={{0,1},{1,0},{2,3},{3,2},{4,5},{5,4},{6,7},{7,6},{8,9},{9,8},{10,11... | collective-permute-start | bytes 5603336 | tf_op jit(solution)/shard_map/ppermute | solution.py:474
  63.1 25.5 %collective-permute-start.19 = (bf16[384,1024]{1,0:T(8,128)(2,1)S(1)}, bf16[384,1024]{1,0:T(8,128)(2,1)}, u32[]{:S(2)}, u32[]{:S(2)}) collective-permute-start(bf16[384,1024]{1,0:T(8,128)(2,1)S(1)} %constant_dynamic-update-slice_fusion.3.refs_4_), channel_id=1, source_target_pairs={{0,16},{1,9},{2,18},{3,11},{4,20},{5,13},{6,22},{7,15},{8,24},{9,1... | collective-permute-start | bytes 2359304 | tf_op jit(solution)/shard_map/ppermute | solution.py:563
  88.6 5.2 %collective-permute-start.21 = (bf16[384,2432]{1,0:T(8,128)(2,1)}, bf16[384,2432]{1,0:T(8,128)(2,1)S(1)}, u32[]{:S(2)}, u32[]{:S(2)}) collective-permute-start(bf16[384,2432]{1,0:T(8,128)(2,1)} %collective-permute-done.18.refs_1_), channel_id=1, source_target_pairs={{0,1},{1,0},{2,3},{3,2},{4,5},{5,4},{6,7},{7,6},{8,9},{9,8},{10,11... | collective-permute-start | bytes 5603336 | tf_op jit(solution)/shard_map/ppermute | solution.py:474
  132.5 30.7 %collective-permute-start.26 = (bf16[2,256,768]{2,1,0:T(8,128)(2,1)}, bf16[2,256,768]{2,1,0:T(8,128)(2,1)S(1)}, u32[]{:S(2)}, u32[]{:S(2)}) collective-permute-start(bf16[2,256,768]{2,1,0:T(8,128)(2,1)} %get-tuple-element.90), channel_id=1, source_target_pairs={{0,1},{1,0},{2,3},{3,2},{4,5},{5,4},{6,7},{7,6},{8,9},{9,8},{10,11... | collective-permute-start | bytes 2359304 | tf_op jit(solution)/shard_map/ppermute | solution.py:474
  158.8 16.5 %collective-permute-start.25 = (f32[16,768]{1,0:T(8,128)}, f32[16,768]{1,0:T(8,128)S(1)}, u32[]{:S(2)}, u32[]{:S(2)}) collective-permute-start(f32[16,768]{1,0:T(8,128)} %get-tuple-element.88), channel_id=1, source_target_pairs={{0,24},{2,26},{4,28},{6,30},{8,16},{10,18},{12,20},{14,22},{16,8},... | collective-permute-start | bytes 147464 | tf_op jit(solution)/shard_map/ppermute | solution.py:482
  160.7 14.6 %collective-permute-start.24 = (f32[16,768]{1,0:T(8,128)}, f32[16,768]{1,0:T(8,128)S(1)}, u32[]{:S(2)}, u32[]{:S(2)}) collective-permute-start(f32[16,768]{1,0:T(8,128)} %get-tuple-element.88), channel_id=1, source_target_pairs={{0,16},{2,18},{4,20},{6,22},{8,24},{10,26},{12,28},{14,30},{16,0},... | collective-permute-start | bytes 147464 | tf_op jit(solution)/shard_map/ppermute | solution.py:482
  160.9 14.4 %collective-permute-start.23 = (f32[16,768]{1,0:T(8,128)}, f32[16,768]{1,0:T(8,128)S(1)}, u32[]{:S(2)}, u32[]{:S(2)}) collective-permute-start(f32[16,768]{1,0:T(8,128)} %get-tuple-element.88), channel_id=1, source_target_pairs={{0,8},{2,10},{4,12},{6,14},{8,0},{10,2},{12,4},{14,6},{16,24},{18,... | collective-permute-start | bytes 147464 | tf_op jit(solution)/shard_map/ppermute | solution.py:482
  175.4 5.1 %collective-permute-start.29 = (f32[16,768]{1,0:T(8,128)S(1)}, f32[16,768]{1,0:T(8,128)S(1)}, u32[]{:S(2)}, u32[]{:S(2)}) collective-permute-start(f32[16,768]{1,0:T(8,128)S(1)} %add_add_fusion.1), channel_id=1, source_target_pairs={{0,6},{2,4},{4,2},{6,0},{8,14},{10,12},{12,10},{14,8},{16,22},{18,... | collective-permute-start | bytes 147464 | tf_op jit(solution)/shard_map/ppermute | solution.py:482
  (31 other events, 301.5 us)
